TPU v7x, 32 devices: a whole 2x2x4 slice. The times are simulated.
32 devices in a mesh: dev: 32 (over z, y, x, core).
Axes of the slice: x: 2, y: 2, z: 4, core: 2. Of those that a mesh axis runs over, the one named last changes fastest.
Arguments:
- table: bfloat16 [32768, 512], P('dev'), may hold values from -6 to 6
- owners: int32 [32768, 4], P('dev'), may hold values from 0 to 31, all different within a row; in each aligned block of 1024 rows (0 to 1023, 1024 to 2047, ...) at most 256 rows name the same one
- local_rows: int32 [32768, 4], P('dev'), may hold values from 0 to 1023
- segments: int32 [32, 1024], P('dev'), may hold values from 0 to 3, never falling along the last dimension, each value on 1 to 512 neighbouring positions
- cotangent: bfloat16 [32768, 512], P('dev'), may hold values from -6 to 6
- weights: bfloat16 [512, 2560], replicated, may hold values from -0.25 to 0.25
- master: float32 [512, 2560], P('dev'), may hold values from -0.25 to 0.25
- moment1: float32 [512, 2560], P('dev'), may hold values from -6 to 6
- moment2: float32 [512, 2560], P('dev'), may hold values from 0.2 to 5
Outputs:
- table_grad: float32 [32768, 512], P('dev')
- new_weights: bfloat16 [512, 2560], replicated
- new_master: float32 [512, 2560], P('dev')
- new_moment1: float32 [512, 2560], P('dev')
- new_moment2: float32 [512, 2560], P('dev')
Inputs may be any that keep to these rules, and one draw needn't show every extreme that they name: Each history row names 4 different owners; within the 1024 rows of one device no owner is named more than 256 times, and that bound is reached on some devices. `segments`: within each row, sequence numbers never fall and each sequence holds 1 to 512 rows.
All inputs are finite; a program needn't handle non-finite values.
Results may differ from a plain program's by a relative error of at most 0.012.
Values may be sent and summed in bfloat16 or wider, within the bound.
No kernel may reach another device: no remote copies, remote signals or barrier semaphores. Data moves between devices by JAX's collectives and lax.ppermute only.
A program may use at most 320 MiB of HBM per device.

v0:
```python
import jax
import jax.numpy as jnp
from jax import lax
from jax.sharding import PartitionSpec as P

HEADS = 8
MAXLEN = 512


def layer_norm(values):
    mean = jnp.mean(values, axis=-1, keepdims=True)
    centred = values - mean
    var = jnp.mean(centred * centred, axis=-1, keepdims=True)
    return centred * lax.rsqrt(var + 1e-05)


def head_attention(query, key, value, mask):
    scores = jnp.dot(query, key.T, preferred_element_type=jnp.float32)
    weight_mat = (jnp.where(mask, jax.nn.silu(scores), 0.0) / MAXLEN).astype(jnp.bfloat16)
    return jnp.dot(weight_mat, value, preferred_element_type=jnp.float32)


def attention_core(pre, segs):
    act = jax.nn.silu(pre).astype(jnp.bfloat16)
    count = pre.shape[0]
    width = act.shape[1] // 4
    gate = act[:, 0:width]
    value = act[:, width : 2 * width]
    query = act[:, 2 * width : 3 * width]
    key = act[:, 3 * width : 4 * width]

    def split_heads(array):
        return array.reshape(count, HEADS, width // HEADS).transpose(1, 0, 2)

    places = jnp.arange(count, dtype=jnp.int32)
    mask = (segs[:, None] == segs[None, :]) & (places[:, None] >= places[None, :])
    heads_out = lax.map(
        lambda trio: head_attention(trio[0], trio[1], trio[2], mask),
        (split_heads(query), split_heads(key), split_heads(value)),
    )
    attended = heads_out.transpose(1, 0, 2).reshape(count, width)
    return (layer_norm(attended) * gate.astype(jnp.float32)).astype(jnp.bfloat16)


def backward_pieces(rows, segs, weights, cotangent):
    width = weights.shape[0]
    rows_f = rows.astype(jnp.float32)
    normed, norm_back = jax.vjp(layer_norm, rows_f)
    normed_b = normed.astype(jnp.bfloat16)
    w_input = weights[:, : 4 * width]
    w_output = weights[:, 4 * width :]
    pre = jnp.dot(normed_b, w_input, preferred_element_type=jnp.float32)
    mixed, core_back = jax.vjp(lambda values: attention_core(values, segs), pre)
    d_mixed = jnp.dot(cotangent, w_output.T, preferred_element_type=jnp.float32).astype(
        jnp.bfloat16
    )
    d_pre = core_back(d_mixed)[0].astype(jnp.bfloat16)
    d_normed = jnp.dot(d_pre, w_input.T, preferred_element_type=jnp.float32)
    d_rows = (norm_back(d_normed)[0] + cotangent.astype(jnp.float32)).astype(jnp.bfloat16)
    return (normed_b, mixed, d_pre, d_rows)


def shards(table, owners, local_rows, segments, cotangent, weights, master, moment1, moment2):
    devices = lax.axis_size("dev")
    count = owners.shape[0]
    feats = owners.shape[1]
    items = count * feats
    width = weights.shape[0]
    capacity = max(2, 2 * feats * count // devices)
    owner_of = owners.reshape(items)
    local_of = local_rows.reshape(items)
    onehot = (owner_of[:, None] == jnp.arange(devices, dtype=jnp.int32)[None, :]).astype(jnp.int32)
    before = jnp.cumsum(onehot, axis=0) - onehot
    rank = jnp.sum(before * onehot, axis=1)
    slot = owner_of * capacity + rank
    outbox = jnp.zeros((devices * capacity,), jnp.int32).at[slot].set(local_of)
    outbox = outbox.reshape(devices, capacity)
    asked = lax.all_to_all(outbox, "dev", split_axis=0, concat_axis=0, tiled=True)
    fetched_rows = table[asked]
    back = lax.all_to_all(fetched_rows, "dev", split_axis=0, concat_axis=0, tiled=True)
    picked = back.reshape(devices * capacity, width)[slot].reshape(count, feats, width)
    rows = jnp.sum(picked.astype(jnp.float32), axis=1).astype(jnp.bfloat16)
    normed_b, mixed, d_pre, d_rows = backward_pieces(rows, segments[0], weights, cotangent)
    spread = jnp.broadcast_to(d_rows[:, None, :], (count, feats, width)).reshape(items, width)
    grad_box = jnp.zeros((devices * capacity, width), jnp.bfloat16).at[slot].set(spread)
    returned = lax.all_to_all(
        grad_box.reshape(devices, capacity, width), "dev", split_axis=0, concat_axis=0, tiled=True
    )
    table_grad = (
        jnp.zeros((table.shape[0], width), jnp.float32)
        .at[asked.reshape(-1)]
        .add(returned.reshape(devices * capacity, width).astype(jnp.float32))
    )
    full_grad = jnp.concatenate(
        [
            jnp.dot(normed_b.T, d_pre, preferred_element_type=jnp.float32),
            jnp.dot(mixed.T, cotangent, preferred_element_type=jnp.float32),
        ],
        axis=1,
    )
    grad = lax.psum_scatter(full_grad, "dev", scatter_dimension=0, tiled=True)
    new_m1 = 0.9 * moment1 + 0.1 * grad
    new_m2 = 0.95 * moment2 + 0.05 * grad * grad
    fix1 = 1.0 - 0.9**10
    fix2 = 1.0 - 0.95**10
    new_master = master - 0.01 * (new_m1 / fix1) / (jnp.sqrt(new_m2 / fix2) + 1e-08)
    new_weights = lax.all_gather(new_master.astype(jnp.bfloat16), "dev", axis=0, tiled=True)
    return (table_grad, new_weights, new_master, new_m1, new_m2)


def solution(mesh):
    return jax.shard_map(
        shards,
        mesh=mesh,
        in_specs=(
            P("dev", None),
            P("dev", None),
            P("dev", None),
            P("dev", None),
            P("dev", None),
            P(),
            P("dev", None),
            P("dev", None),
            P("dev", None),
        ),
        out_specs=(P("dev", None), P(), P("dev", None), P("dev", None), P("dev", None)),
        check_vma=False,
    )
```

profile of v0, /device:TPU:0, one launch (start us, length us, event | category | flops | bytes accessed | tf_op | source)
XLA Modules:
  0.0 913.1 jit_solution(14092615965524045226)
XLA Ops:
  9.5 9.2 %reduce-window.6 = s32[32,32,128]{2,1,0:T(8,128)S(1)} reduce-window(s32[32,32,128]{2,1,0:T(8,128)S(1)} %fusion.80, s32[]{:T(128)} %copy.100), window={size=1x1x128 pad=0_0x0_0x127_0}, to_apply=%region_0.0 | reduce-window | flops 16646144 | bytes 1048580 | tf_op jit(solution)/shard_map/reduce-window
  21.5 15.5 %scatter_custom_fusion = s32[8192]{0:T(1024)S(1)} fusion(s32[4096]{0:T(1024)S(1)} %bitcast.217, s32[4096]{0:T(1024)S(1)} %reshape.253, s32[]{:T(128)} %copy.100), kind=kCustom, calls=%fused_computation.124 | custom fusion | bytes 32772 | tf_op jit(solution)/shard_map/scatter | solution.py:76
  37.0 14.4 %all_to_all.22 = s32[32,1,256]{2,1,0:T(1,128)S(1)} all-to-all(s32[32,1,256]{2,1,0:T(1,128)S(1)} %bitcast.213), channel_id=1, replica_groups=mesh['dev'=32] {'dev'}, dimensions={0} | all-to-all | bytes 65536 | tf_op jit(solution)/shard_map/all_to_all | solution.py:78
  52.1 33.5 %gather_fusion = bf16[8192,512]{1,0:T(8,128)(2,1)} fusion(bf16[1024,512]{1,0:T(8,128)(2,1)S(1)} %copy-done, s32[8192]{0:T(1024)S(1)} %broadcast_clamp_fusion), kind=kCustom, calls=%fused_computation | custom fusion | bytes 16809984 | tf_op jit(solution)/shard_map/gather | solution.py:79
  85.6 3.8 all-to-all-start.1
  91.1 184.4 %all-to-all-done.1 = bf16[32,256,512]{2,1,0:T(8,128)(2,1)} async-done(((bf16[32,256,512]{2,1,0:T(8,128)(2,1)}), bf16[32,256,512]{2,1,0:T(8,128)(2,1)}, u32[]{:S(2)}, u32[]{:S(2)}) %all-to-all-start.1) | async-done | bytes 8388640 | tf_op jit(solution)/shard_map/all_to_all | solution.py:80
  275.5 21.8 %gather_fusion.1 = bf16[4096,512]{1,0:T(8,128)(2,1)} fusion(bf16[8192,512]{1,0:T(8,128)(2,1)} %bitcast.9, s32[4096]{0:T(1024)S(1)} %broadcast_clamp_fusion.1), kind=kCustom, calls=%fused_computation.1 | custom fusion | bytes 8404992 | tf_op jit(solution)/shard_map/gather | solution.py:81
  297.3 6.9 reshape.221
  304.3 8.2 reduce_sum.113
  314.5 7.4 multiply_convert_fusion.2
  331.1 106.9 %while.41 = (s32[]{:T(128)}, f32[8,1024,64]{1,2,0:T(8,128)S(1)}, bf16[8,64,1024]{2,1,0:T(8,128)(2,1)}, f32[8,1024,1024]{2,1,0:T(8,128)}, f32[8,1024,1024]{2,1,0:...) while((s32[]{:T(128)}, f32[8,1024,64]{1,2,0:T(8,128)S(1)}, ...), condition=%wide.region_8.9_spmd.clone, body=%wide.region_7.8_spmd.clone.sunk | while | flops 294649856 | bytes 28462708 | solution.py:37
  331.3 6.7 bitcast_dynamic-update-slice_fusion.7
  340.1 2.9 bitcast_dynamic-update-slice_fusion.9
  344.6 6.7 bitcast_dynamic-update-slice_fusion.7
  353.3 3.0 bitcast_dynamic-update-slice_fusion.9
  357.9 6.7 bitcast_dynamic-update-slice_fusion.7
  366.7 3.0 bitcast_dynamic-update-slice_fusion.9
  371.3 6.7 bitcast_dynamic-update-slice_fusion.7
  380.0 3.0 bitcast_dynamic-update-slice_fusion.9
  384.6 6.7 bitcast_dynamic-update-slice_fusion.7
  393.4 3.0 bitcast_dynamic-update-slice_fusion.9
  397.9 6.7 bitcast_dynamic-update-slice_fusion.7
  406.7 3.0 bitcast_dynamic-update-slice_fusion.9
  411.2 6.8 bitcast_dynamic-update-slice_fusion.7
  420.1 3.0 bitcast_dynamic-update-slice_fusion.9
  424.6 6.7 bitcast_dynamic-update-slice_fusion.7
  433.4 2.9 bitcast_dynamic-update-slice_fusion.9
  450.6 103.4 %while.42 = (s32[]{:T(128)}, bf16[8,1024,64]{1,2,0:T(8,128)(2,1)}, bf16[8,1024,64]{1,2,0:T(8,128)(2,1)}, bf16[8,1024,64]{1,2,0:T(8,128)(2,1)}, bf16[8,1024,64]{2...) while((s32[]{:T(128)}, bf16[8,1024,64]{1,2,0:T(8,128)(2,1)}, ...), condition=%wide.region_14.15_spmd.clone, body=%wide.region_13.14_spmd.clone.sunk | while | flops 548405248 | bytes 22557848 | solution.py:37
  450.6 5.7 fusion.122
  463.5 5.7 fusion.122
  476.4 5.7 fusion.122
  486.6 2.8 fusion.125
  489.4 5.7 fusion.122
  502.3 5.7 fusion.122
  515.2 5.7 fusion.122
  528.1 5.7 fusion.122
  538.3 2.8 fusion.125
  541.1 5.7 fusion.122
  554.0 6.7 fusion.52
  570.1 2.9 add_convert_fusion
  574.5 3.0 broadcast_in_dim.132
  577.6 7.0 reshape.261
  584.5 23.6 %scatter_custom_fusion.1 = bf16[8192,512]{1,0:T(8,128)(2,1)} fusion(s32[4096]{0:T(1024)} %bitcast.219, bf16[4096,512]{1,0:T(8,128)(2,1)} %reshape.261, bf16[]{:T(256)} %constant.153.clone.1), kind=kCustom, calls=%fused_computation.72 | custom fusion | bytes 8389120 | tf_op jit(solution)/shard_map/scatter | solution.py:85
  608.2 3.8 all-to-all-start.2
  612.1 150.5 %reduce-scatter.2.cloned.1.call-done = f32[16,2560]{1,0:T(8,128)} async-done(((f32[512,2560]{1,0:T(8,128)}), f32[16,2560]{1,0:T(8,128)}) %reduce-scatter.2.cloned.1.call-update) | async-done | bytes 163856 | tf_op jit(solution)/shard_map/reduce_scatter | solution.py:101
  764.4 81.3 %all-gather.2.cloned.1.call-done = bf16[512,2560]{1,0:T(8,128)(2,1)} async-done(((bf16[16,2560]{1,0:T(8,128)(2,1)}), bf16[512,2560]{1,0:T(8,128)(2,1)}) %all-gather.2.cloned.1.call-update) | async-done | bytes 2621456 | tf_op jit(solution)/shard_map/all_gather | solution.py:107
  845.8 56.9 %scatter_custom_fusion.2 = f32[1024,512]{1,0:T(8,128)} fusion(s32[8192]{0:T(1024)S(1)} %bitcast.220, bf16[8192,512]{1,0:T(8,128)(2,1)} %bitcast.55, f32[]{:T(128)} %constant.148.clone.1), kind=kCustom, calls=%fused_computation.61 | custom fusion | flops 8388608 | bytes 10485764 | tf_op jit(solution)/shard_map/scatter-add | solution.py:92
  902.7 3.4 copy.101
  (133 shorter events, 125.2 us)
Async XLA Ops:
  7.2 44.9 %copy-start = (bf16[1024,512]{1,0:T(8,128)(2,1)S(1)}, bf16[1024,512]{1,0:T(8,128)(2,1)}, u32[]{:S(2)}) copy-start(bf16[1024,512]{1,0:T(8,128)(2,1)} %param.13) | copy-start | bytes 3145732
  7.2 13.4 %copy-start.16 = (s32[1024,4]{0,1:T(4,128)S(1)}, s32[1024,4]{0,1:T(4,128)}, u32[]{:S(2)}) copy-start(s32[1024,4]{0,1:T(4,128)} %param.15) | copy-start | bytes 49156
  21.5 69.6 %copy-start.13 = (s32[4096,1]{0,1:T(1,128)}, s32[4096,1]{0,1:T(1,128)S(1)}, u32[]{:S(2)}) copy-start(s32[4096,1]{0,1:T(1,128)S(1)} %compare_select_fusion.2) | copy-start | bytes 49156
  51.4 0.6 copy-start.8
  85.6 4.1 copy-start.5
  85.6 189.9 %all-to-all-start.1 = ((bf16[32,256,512]{2,1,0:T(8,128)(2,1)}), bf16[32,256,512]{2,1,0:T(8,128)(2,1)}, u32[]{:S(2)}, u32[]{:S(2)}) async-start(bf16[32,256,512]{2,1,0:T(8,128)(2,1)} %bitcast.199), calls=%async_computation.1 | async-start | bytes 16777216 | tf_op jit(solution)/shard_map/all_to_all | solution.py:80
  89.5 673.1 %reduce-scatter.2.cloned.1.call-start = ((), (), s32[]{:S(2)}) async-start(), calls=%async_computation.4 | async-start | bytes 5406720 | tf_op jit(solution)/shard_map/reduce_scatter | solution.py:101
  314.5 7.4 copy-start.14
  322.0 1.9 copy-start.2
  325.6 5.4 copy-start.4
  438.1 3.0 copy-start.3
  560.7 2.4 copy-start.17
  563.1 2.4 copy-start.6
  563.1 2.4 copy-start.7
  568.9 0.7 copy-start.15
  608.1 154.4 %copy-start.10 = (f32[16,2560]{1,0:T(8,128)S(1)}, f32[16,2560]{1,0:T(8,128)}, u32[]{:S(2)}) copy-start(f32[16,2560]{1,0:T(8,128)} %param.19) | copy-start | bytes 491524
  608.2 154.4 %copy-start.11 = (f32[16,2560]{1,0:T(8,128)S(1)}, f32[16,2560]{1,0:T(8,128)}, u32[]{:S(2)}) copy-start(f32[16,2560]{1,0:T(8,128)} %param.20) | copy-start | bytes 491524
  608.2 154.4 %copy-start.12 = (f32[16,2560]{1,0:T(8,128)S(1)}, f32[16,2560]{1,0:T(8,128)}, u32[]{:S(2)}) copy-start(f32[16,2560]{1,0:T(8,128)} %param.21) | copy-start | bytes 491524
  608.2 156.2 %copy-start.9 = (s32[32,1,256]{2,1,0:T(1,128)S(1)}, s32[32,1,256]{2,1,0:T(1,128)}, u32[]{:S(2)}) copy-start(s32[32,1,256]{2,1,0:T(1,128)} %copy-done.8) | copy-start | bytes 98308
  608.2 237.6 %all-to-all-start.2 = ((bf16[32,256,512]{2,1,0:T(8,128)(2,1)}), bf16[32,256,512]{2,1,0:T(8,128)(2,1)}, u32[]{:S(2)}, u32[]{:S(2)}) async-start(bf16[32,256,512]{2,1,0:T(8,128)(2,1)} %bitcast.200), calls=%async_computation.2 | async-start | bytes 16777216 | tf_op jit(solution)/shard_map/all_to_all | solution.py:86
  612.0 233.7 %all-gather.2.cloned.1.call-start = ((), (), s32[]{:S(2)}) async-start(), calls=%async_computation.5 | async-start | bytes 2703360 | tf_op jit(solution)/shard_map/all_gather | solution.py:107
  845.8 60.3 %copy-start.1 = (bf16[1024,512]{1,0:T(8,128)(2,1)S(1)}, bf16[1024,512]{1,0:T(8,128)(2,1)}, u32[]{:S(2)}) copy-start(bf16[1024,512]{1,0:T(8,128)(2,1)} %param.13) | copy-start | bytes 3145732
Sparse Core Ops, SparseCore 0:
  569.1 193.4 reduce-scatter.1
  766.0 79.7 all-gather.1
where the time goes:
time: 919 us; the launch traced here: 913 us
  waiting for transfers between devices  416 us (45%)
  matrix products  189 us (21%)
  local copies, waits for them, and re-layouts  151 us (16%)
  other arithmetic  119 us (13%)
  between operations  14.7 us (2%)
  blocking collectives  14.4 us (2%)
    all_to_all x1, waiting for transfers between devices, shards(): lax.all_to_all(fetched_rows, 'dev', split_axis=0, concat_axis=0, tiled=True)  184 us
    reduce_scatter x1, waiting for transfers between devices, shards(): grad = lax.psum_scatter(full_grad, 'dev', scatter_dimension=0, tiled=True)  150 us
    dot_general x24, matrix products, head_attention(): scores = jnp.dot(query, key.T, preferred_element_type=jnp.float32)  89.2 us
    dot_general x24, matrix products, head_attention(): return jnp.dot(weight_mat, value, preferred_element_type=jnp.float32)  84.4 us
    all_gather x1, waiting for transfers between devices, shards(): lax.all_gather(new_master.astype(jnp.bfloat16), 'dev', axis=0, tiled=True)  81.3 us
    scatter-add x1, other arithmetic, shards(): table_grad = jnp.zeros((table.shape[0], width), jnp.float32).at[asked.res...  56.9 us
    gather x1, local copies, waits for them, and re-layouts, shards(): fetched_rows = table[asked]  33.5 us
    dynamic_update_slice x8, other arithmetic, attention_core(): lax.map(lambda trio: head_attention(trio[0], trio[1], trio[2], mask), (sp...  23.8 us
  transfers between devices with their start and end apart: 4, of which 3 were waited for; matrix products, arithmetic and copies ran while one was open for 5% of the time, Pallas kernels for 0%

commit v1 on v0

v1 whole, which is shorter than its diff:
```python
import functools
import jax
import jax.numpy as jnp
from jax import lax
from jax.experimental import pallas as pl
from jax.experimental.pallas import tpu as pltpu
from jax.sharding import PartitionSpec as P

HEADS = 8
MAXLEN = 512
F32 = jnp.float32
BF16 = jnp.bfloat16
LANES = 128


def sigmoid(v):
    return 0.5 * jnp.tanh(0.5 * v) + 0.5


def nt(a, b):
    return lax.dot_general(a, b, (((1,), (1,)), ((), ())), preferred_element_type=F32)


def nn(a, b):
    return jnp.dot(a, b, preferred_element_type=F32)


def row_stats(v):
    mean = jnp.mean(v, axis=-1, keepdims=True)
    cen = v - mean
    var = jnp.mean(cen * cen, axis=-1, keepdims=True)
    rstd = lax.rsqrt(var + 1e-05)
    return cen * rstd, rstd


def norm_grad(hat, rstd, dy):
    m1 = jnp.mean(dy, axis=-1, keepdims=True)
    m2 = jnp.mean(dy * hat, axis=-1, keepdims=True)
    return rstd * (dy - m1 - hat * m2)


def dense_body(block, splits, *refs):
    x_refs, (segc_ref, segr_ref, w_ref, cot_ref) = refs[:splits], refs[splits:splits + 4]
    dx_refs, refs = refs[splits + 4:2 * splits + 4], refs[2 * splits + 4:]
    (normed_ref, mixed_ref, dpre_ref, mask, dsil, act, dmix, att, datt, wsave, dsave, dvt, dkt) = refs
    rows, width = cot_ref.shape
    wide = width // splits
    head = width // HEADS
    lanes = 2 * head
    npair = HEADS // 2
    nblk = rows // block
    band = -(-MAXLEN // block)
    tiles = [(q, k) for q in range(nblk) for k in range(max(0, q - band), q + 1)]
    where = {t: i for i, t in enumerate(tiles)}

    def rs(i):
        return pl.ds(pl.multiple_of(i * block, block), block)

    def x_rows(r):
        return jnp.concatenate([v[r, :] for v in x_refs], axis=1).astype(F32)

    def first(i, c):
        r = rs(i)
        hat, _ = row_stats(x_rows(r))
        nb = hat.astype(BF16)
        normed_ref[r, :] = nb
        for j in range(4):
            cols = slice(j * width, (j + 1) * width)
            pre = nn(nb, w_ref[:, cols])
            sg = sigmoid(pre)
            a = pre * sg
            act[r, cols] = a.astype(BF16)
            dsil[r, cols] = sg + a * (1.0 - sg)
        dmix[r, :] = nt(cot_ref[r, :], w_ref[:, 4 * width:]).astype(BF16)
        return c

    lax.fori_loop(0, nblk, first, 0)

    for j, (q, k) in enumerate(tiles):
        same = segc_ref[q * block:(q + 1) * block, :] == segr_ref[:, k * block:(k + 1) * block]
        if q == k:
            ri = lax.broadcasted_iota(jnp.int32, (block, block), 0)
            ci = lax.broadcasted_iota(jnp.int32, (block, block), 1)
            same = same & (ri >= ci)
        mask[j] = jnp.where(same, 1.0 / MAXLEN, 0.0)

    low = lax.broadcasted_iota(jnp.int32, (block, lanes), 1) < head

    def halves(v):
        zero = jnp.zeros_like(v)
        return jnp.where(low, v, zero), jnp.where(low, zero, v)

    def cols(part, p):
        return pl.ds(pl.multiple_of(part * width + p * lanes, lanes), lanes)

    def forward(p, c):
        for q in range(nblk):
            qr = slice(q * block, (q + 1) * block)
            qh = halves(act[qr, cols(2, p)])
            acc = jnp.zeros((block, lanes), F32)
            for k in range(max(0, q - band), q + 1):
                kr = slice(k * block, (k + 1) * block)
                j = where[(q, k)]
                key = act[kr, cols(3, p)]
                vh = halves(act[kr, cols(1, p)])
                for h in range(2):
                    s = nt(qh[h], key)
                    m = mask[j]
                    sg = sigmoid(s)
                    a = s * sg
                    wt = (a * m).astype(BF16)
                    wsave[p * 2 + h, j] = wt
                    dsave[p * 2 + h, j] = ((sg + a * (1.0 - sg)) * m).astype(BF16)
                    acc += nn(wt, vh[h])
            att[qr, cols(0, p)] = acc
        return c

    lax.fori_loop(0, npair, forward, 0)

    def middle(i, c):
        r = rs(i)
        hat, rstd = row_stats(att[r, :])
        g = act[r, 0:width].astype(F32)
        dm = dmix[r, :].astype(F32)
        mixed_ref[r, :] = (hat * g).astype(BF16)
        dgate = (dm * hat).astype(BF16).astype(F32)
        dpre_ref[r, 0:width] = (dgate * dsil[r, 0:width]).astype(BF16)
        datt[r, :] = norm_grad(hat, rstd, dm * g).astype(BF16)
        return c

    lax.fori_loop(0, nblk, middle, 0)

    def backward(p, c):
        dvt[...] = jnp.zeros(dvt.shape, F32)
        dkt[...] = jnp.zeros(dkt.shape, F32)
        for q in range(nblk):
            qr = slice(q * block, (q + 1) * block)
            da = datt[qr, cols(0, p)]
            qv = act[qr, cols(2, p)]
            dh = halves(da)
            dat = da.astype(F32).T.astype(BF16)
            qt = qv.astype(F32).T.astype(BF16)
            acc = jnp.zeros((block, lanes), F32)
            for k in range(max(0, q - band), q + 1):
                kr = slice(k * block, (k + 1) * block)
                j = where[(q, k)]
                val = act[kr, cols(1, p)]
                kh = halves(act[kr, cols(3, p)])
                for h in range(2):
                    hr = slice(h * head, (h + 1) * head)
                    dw = nt(dh[h], val).astype(BF16).astype(F32)
                    ds = (dw * dsave[p * 2 + h, j].astype(F32)).astype(BF16)
                    acc += nn(ds, kh[h])
                    dvt[hr, kr] += nn(dat[hr, :], wsave[p * 2 + h, j])
                    dkt[hr, kr] += nn(qt[hr, :], ds)
            dq = acc.astype(BF16).astype(F32)
            dpre_ref[qr, cols(2, p)] = (dq * dsil[qr, cols(2, p)]).astype(BF16)
        for k in range(nblk):
            kr = slice(k * block, (k + 1) * block)
            dv = dvt[:, kr].T.astype(BF16).astype(F32)
            dk = dkt[:, kr].T.astype(BF16).astype(F32)
            dpre_ref[kr, cols(1, p)] = (dv * dsil[kr, cols(1, p)]).astype(BF16)
            dpre_ref[kr, cols(3, p)] = (dk * dsil[kr, cols(3, p)]).astype(BF16)
        return c

    lax.fori_loop(0, npair, backward, 0)

    def last(i, c):
        r = rs(i)
        hat, rstd = row_stats(x_rows(r))
        dn = nt(dpre_ref[r, :], w_ref[:, 0:4 * width])
        dx = norm_grad(hat, rstd, dn) + cot_ref[r, :].astype(F32)
        for n, ref in enumerate(dx_refs):
            ref[r, :] = dx[:, n * wide:(n + 1) * wide].astype(BF16)
        return c

    lax.fori_loop(0, nblk, last, 0)


def dense(x, segs, weights, cot):
    splits = len(x)
    rows, width = cot.shape
    block = min(256, rows)
    nblk = rows // block
    band = -(-MAXLEN // block)
    ntile = sum(min(q, band) + 1 for q in range(nblk))
    lanes = 2 * width // HEADS
    vm = pl.BlockSpec(memory_space=pltpu.VMEM)
    return pl.pallas_call(
        functools.partial(dense_body, block, splits),
        out_shape=(jax.ShapeDtypeStruct((rows, width // splits), BF16),) * splits
        + (
            jax.ShapeDtypeStruct((rows, width), BF16),
            jax.ShapeDtypeStruct((rows, width), BF16),
            jax.ShapeDtypeStruct((rows, 4 * width), BF16),
        ),
        in_specs=[vm] * (splits + 4),
        out_specs=(vm,) * (splits + 3),
        scratch_shapes=[
            pltpu.VMEM((ntile, block, block), F32),
            pltpu.VMEM((rows, 4 * width), F32),
            pltpu.VMEM((rows, 4 * width), BF16),
            pltpu.VMEM((rows, width), BF16),
            pltpu.VMEM((rows, width), F32),
            pltpu.VMEM((rows, width), BF16),
            pltpu.VMEM((HEADS, ntile, block, block), BF16),
            pltpu.VMEM((HEADS, ntile, block, block), BF16),
            pltpu.VMEM((lanes, rows), F32),
            pltpu.VMEM((lanes, rows), F32),
        ],
        compiler_params=pltpu.CompilerParams(vmem_limit_bytes=60 * 1024 * 1024),
        name="dense_step",
    )(*x, segs.reshape(rows, 1), segs.reshape(1, rows), weights, cot)


def spread_rows(dst, base, src, chunk):
    rows, width = src.shape
    parts = width // LANES

    def step(i, c):
        for j in range(parts):
            piece = src[pl.ds(pl.multiple_of(i * chunk, chunk), chunk), j * LANES:(j + 1) * LANES]
            start = pl.multiple_of(base * parts + i * (chunk * parts), 8) + j
            dst[pl.ds(start, chunk, stride=parts), :] = piece.astype(F32)
        return c

    lax.fori_loop(0, rows // chunk, step, 0)


def join_rows(dst, src, base, chunk):
    rows, width = dst.shape
    parts = width // LANES

    def step(i, c):
        for j in range(parts):
            start = pl.multiple_of(base * parts + i * (chunk * parts), 8) + j
            piece = src[pl.ds(start, chunk, stride=parts), :]
            dst[pl.ds(pl.multiple_of(i * chunk, chunk), chunk), j * LANES:(j + 1) * LANES] = piece.astype(dst.dtype)
        return c

    lax.fori_loop(0, rows // chunk, step, 0)


def gather_body(ntab, unroll, idx, *refs):
    tabs, out, tab, acc = refs[:ntab], refs[ntab], refs[ntab + 1], refs[ntab + 2]
    rows, width = tabs[0].shape
    parts = width // LANES
    count = out.shape[0]
    feats = idx.shape[0] // count
    chunk = 64
    for i in range(ntab):
        spread_rows(tab, i * rows, tabs[i], chunk)
    tab[pl.ds(ntab * rows * parts, 8), :] = jnp.zeros((8, LANES), F32)

    def step(i, c):
        for u in range(unroll):
            t = i * unroll + u
            total = tab[pl.ds(idx[t], parts), :]
            for f in range(1, feats):
                total = total + tab[pl.ds(idx[f * count + t], parts), :]
            acc[pl.ds(t * parts, parts), :] = total
        return c

    lax.fori_loop(0, count // unroll, step, 0)
    join_rows(out, acc, 0, chunk)


def gather_sum(idx, tabs, dtype, count):
    rows, width = tabs[0].shape
    parts = width // LANES
    vm = pl.BlockSpec(memory_space=pltpu.VMEM)
    return pl.pallas_call(
        functools.partial(gather_body, len(tabs), 8),
        out_shape=jax.ShapeDtypeStruct((count, width), dtype),
        in_specs=[pl.BlockSpec(memory_space=pltpu.SMEM)] + [vm] * len(tabs),
        out_specs=vm,
        scratch_shapes=[
            pltpu.VMEM((len(tabs) * rows * parts + 8, LANES), F32),
            pltpu.VMEM((count * parts, LANES), F32),
        ],
        compiler_params=pltpu.CompilerParams(vmem_limit_bytes=60 * 1024 * 1024),
        name="gather_sum",
    )(idx, *tabs)


def scatter_body(npiece, nout, unroll, idx, *refs):
    pieces, outs, acc, stage = refs[:npiece], refs[npiece:npiece + nout], refs[-2], refs[-1]
    count, width = pieces[0].shape
    rows = outs[0].shape[0]
    parts = width // LANES
    feats = idx.shape[0] // (npiece * count)
    chunk = 64

    def clear(i, c):
        acc[pl.ds(pl.multiple_of(i * 256, 256), 256), :] = jnp.zeros((256, LANES), F32)
        return c

    lax.fori_loop(0, nout * rows * parts // 256, clear, 0)
    acc[pl.ds(nout * rows * parts, parts * feats), :] = jnp.zeros((parts * feats, LANES), F32)
    for n in range(npiece):
        spread_rows(stage, 0, pieces[n], chunk)

        def step(i, c):
            for u in range(unroll):
                t = i * unroll + u
                val = stage[pl.ds(t * parts, parts), :]
                at = [idx[(n * feats + f) * count + t] for f in range(feats)]
                got = [acc[pl.ds(a, parts), :] for a in at]
                for a, g in zip(at, got):
                    acc[pl.ds(a, parts), :] = g + val
            return c

        lax.fori_loop(0, count // unroll, step, 0)
    for o in range(nout):
        join_rows(outs[o], acc, o * rows, chunk)


def scatter_add(idx, pieces, nout, rows, dtypes):
    count, width = pieces[0].shape
    feats = idx.shape[0] // (len(pieces) * count)
    parts = width // LANES
    vm = pl.BlockSpec(memory_space=pltpu.VMEM)
    return pl.pallas_call(
        functools.partial(scatter_body, len(pieces), nout, 4),
        out_shape=tuple(jax.ShapeDtypeStruct((rows, width), d) for d in dtypes),
        in_specs=[pl.BlockSpec(memory_space=pltpu.SMEM)] + [vm] * len(pieces),
        out_specs=(vm,) * nout,
        scratch_shapes=[
            pltpu.VMEM(((nout * rows + feats) * parts, LANES), F32),
            pltpu.VMEM((count * parts, LANES), F32),
        ],
        compiler_params=pltpu.CompilerParams(vmem_limit_bytes=60 * 1024 * 1024),
        name="scatter_add",
    )(idx, *pieces)


SPLITS = 2
GROUP_BYTES = 16 * 1024 * 1024


def swap(v, bits):
    devices = lax.axis_size("dev")
    return lax.ppermute(v, "dev", [(i, i ^ bits) for i in range(devices)])


def sum_grad(grad, me, devices, block_rows):
    bits = devices.bit_length() - 1
    v = grad.reshape((2,) * bits + (block_rows, grad.shape[1]))
    for b in range(bits):
        axis = bits - 1 - b
        mine = (me >> b) & 1
        keep = lax.dynamic_index_in_dim(v, mine, axis, keepdims=False)
        give = lax.dynamic_index_in_dim(v, 1 - mine, axis, keepdims=False)
        v = keep + swap(give.astype(BF16), 1 << b).astype(F32)
    return v


def share_weights(v, me, devices):
    bits = devices.bit_length() - 1
    v = v[None]
    for b in reversed(range(bits)):
        got = swap(v, 1 << b)
        high = ((me >> b) & 1) == 1
        low_half = jnp.where(high, got, v)
        high_half = jnp.where(high, v, got)
        v = jnp.stack([low_half, high_half], axis=1).reshape((-1,) + v.shape[1:])
    return v


def shards(table, owners, local_rows, segments, cotangent, weights, master, moment1, moment2):
    devices = lax.axis_size("dev")
    me = lax.axis_index("dev")
    count, feats = owners.shape
    rows, width = table.shape
    wide = width // SPLITS
    parts = wide // LANES
    group = 1
    while group < devices and 2 * group * rows * width * 4 <= GROUP_BYTES:
        group *= 2
    columns = devices // group
    in_group = me % group
    column = me // group

    ids = (owners * rows + local_rows).T
    all_ids = [ids] + [swap(ids, k * group) for k in range(1, columns)]

    def places(v, spare):
        owner = v // rows
        place = ((owner % group) ^ in_group) * rows + v % rows
        return jnp.where(owner // group == column, place, spare) * parts

    x = []
    tabs = []
    for n in range(SPLITS):
        t = [None] * group
        t[0] = table[:, n * wide:(n + 1) * wide]
        for m in range(2, group, 2):
            t[m] = swap(t[0], m)
        tabs.append(t)
    sums = None
    for n in range(SPLITS):
        t = tabs[n]
        if sums is not None:
            sums, t = lax.optimization_barrier((sums, t))
        for m in range(0, group, 2):
            t[m + 1] = swap(t[m], 1)
        sums = [None] * columns
        for k in reversed(range(columns)):
            index = places(all_ids[k], group * rows).reshape(-1)
            sums[k] = gather_sum(index, t, BF16 if k else F32, count)
        total = sums[0]
        for k in range(1, columns):
            total = total + swap(sums[k], k * group).astype(F32)
        x.append(total.astype(BF16))

    out = dense(x, segments[0], weights, cotangent)
    dx, (normed, mixed, d_pre) = out[:SPLITS], out[SPLITS:]

    spare = group * rows + jnp.arange(feats, dtype=jnp.int32)[:, None]
    index = jnp.stack([places(v, spare) for v in all_ids]).reshape(-1)
    halves = []
    for n in range(SPLITS):
        pieces = [dx[n]] + [swap(dx[n], k * group) for k in range(1, columns)]
        outs = scatter_add(index, pieces, group, rows, (F32,) + (BF16,) * (group - 1))
        merged = []
        for m in range(0, group, 2):
            merged.append(outs[m].astype(F32) + swap(outs[m + 1], 1).astype(F32))
        total = merged[0]
        for i, m in enumerate(range(2, group, 2)):
            total = total + swap(merged[i + 1].astype(BF16), m).astype(F32)
        halves.append(total)
    table_grad = jnp.concatenate(halves, axis=1)

    grad_in = jnp.dot(normed.T, d_pre, preferred_element_type=F32)
    grad_out = jnp.dot(mixed.T, cotangent, preferred_element_type=F32)
    full_grad = jnp.concatenate([grad_in, grad_out], axis=1)
    grad = sum_grad(full_grad, me, devices, master.shape[0])
    new_m1 = 0.9 * moment1 + 0.1 * grad
    new_m2 = 0.95 * moment2 + 0.05 * grad * grad
    fix1 = 1.0 - 0.9**10
    fix2 = 1.0 - 0.95**10
    new_master = master - 0.01 * (new_m1 / fix1) / (jnp.sqrt(new_m2 / fix2) + 1e-08)
    new_weights = share_weights(new_master.astype(BF16), me, devices).reshape(weights.shape)
    return (table_grad, new_weights, new_master, new_m1, new_m2)


def solution(mesh):
    split = P("dev", None)
    return jax.shard_map(
        shards,
        mesh=mesh,
        in_specs=(split,) * 5 + (P(),) + (split,) * 3,
        out_specs=(split, P()) + (split,) * 3,
        check_vma=False,
    )
```

time: 919 us -> 492 us (0.54)
  the two profiles are of different devices: /device:TPU:0 before, /device:TPU:8 now
where the time goes in v1:
time: 492 us; the launch traced here: 491 us
  waiting for transfers between devices  209 us (42%)
  Pallas kernels  182 us (37%)
  starting transfers between devices  55.9 us (11%)
  other arithmetic  20.1 us (4%)
  local copies, waits for them, and re-layouts  17.1 us (3%)
  matrix products  5.77 us (1%)
    ppermute x53, waiting for transfers between devices, swap(): return lax.ppermute(v, 'dev', [(i, i ^ bits) for i in range(devices)])  209 us
    pallas_call x2, Pallas kernels, scatter_add(): pl.pallas_call(functools.partial(scatter_body, len(pieces), nout, 4), out...  73.4 us
    pallas_call x8, Pallas kernels, gather_sum(): pl.pallas_call(functools.partial(gather_body, len(tabs), 8), out_shape=ja...  64.9 us
    ppermute x53, starting transfers between devices, swap(): return lax.ppermute(v, 'dev', [(i, i ^ bits) for i in range(devices)])  55.9 us
    pallas_call x1, Pallas kernels, dense(): pl.pallas_call(functools.partial(dense_body, block, splits), out_shape=(j...  43.4 us
    unnamed x91, local copies, waits for them, and re-layouts  12.7 us
  transfers between devices with their start and end apart: 53, of which 21 were waited for; matrix products, arithmetic and copies ran while one was open for 3% of the time, Pallas kernels for 28%

profile of v1, /device:TPU:8, one launch (start us, length us, event | category | flops | bytes accessed | tf_op | source)
XLA Modules:
  0.0 491.2 jit_solution(15719039755406164894)
XLA Ops:
  5.5 11.3 %collective-permute-done.4.refs_2_ = bf16[1024,256]{1,0:T(8,128)(2,1)S(1)} collective-permute-done((bf16[1024,256]{1,0:T(8,128)(2,1)S(1)}, bf16[1024,256]{1,0:T(8,128)(2,1)S(1)}, u32[]{:S(2)}, u32[]{:S(2)}) %collective-permute-start.4) | collective-permute-done | bytes 524320 | tf_op jit(solution)/shard_map/ppermute | solution.py:343
  17.0 3.7 collective-permute-done
  20.7 2.6 collective-permute-start.1
  23.3 2.0 collective-permute-done.1
  36.8 8.1 %gather_sum.9 = bf16[1024,256]{1,0:T(8,128)(2,1)} custom-call(s32[4096]{0:T(1024)} %bitcast.116, bf16[1024,256]{1,0:T(8,128)(2,1)} %copy-done.2, bf16[1024,256]{1,0:T(8,128)(2,1)} %collective-permute-done.3.refs_1_, bf16[1024,256]{1,0:T(8,128)(2,1)} %copy-done.4, bf16[1024,256]{1,0:T(8,128)(2,1)} %collective-permute-done.5.refs_3_, ...), custom_call_target="tpu_custom_call" | custom-call | tf_op jit(solution)/shard_map/gather_sum/pallas_call | solution.py:272
  44.8 8.2 %gather_sum.8 = f32[1024,256]{1,0:T(8,128)} custom-call(s32[4096]{0:T(1024)} %bitcast.114, bf16[1024,256]{1,0:T(8,128)(2,1)} %copy-done.2, bf16[1024,256]{1,0:T(8,128)(2,1)} %collective-permute-done.3.refs_1_, bf16[1024,256]{1,0:T(8,128)(2,1)} %copy-done.4, bf16[1024,256]{1,0:T(8,128)(2,1)} %collective-permute-done.5.refs_3_, bf16[1024,256]{1,0:T(8,128)(2,1)} %copy-done.5, ...), custom_call_target="tpu_custom_call" | custom-call | tf_op jit(solution)/shard_map/gather_sum/pallas_call | solution.py:272
  53.0 8.1 %gather_sum.10 = bf16[1024,256]{1,0:T(8,128)(2,1)} custom-call(s32[4096]{0:T(1024)} %bitcast.118, bf16[1024,256]{1,0:T(8,128)(2,1)} %copy-done.2, bf16[1024,256]{1,0:T(8,128)(2,1)} %collective-permute-done.3.refs_1_, bf16[1024,256]{1,0:T(8,128)(2,1)} %copy-done.4, bf16[1024,256]{1,0:T(8,128)(2,1)} %collective-permute-done.5.refs_3_, ...), custom_call_target="tpu_custom_call" | custom-call | tf_op jit(solution)/shard_map/gather_sum/pallas_call | solution.py:272
  61.1 8.1 %gather_sum.11 = bf16[1024,256]{1,0:T(8,128)(2,1)} custom-call(s32[4096]{0:T(1024)} %bitcast.120, bf16[1024,256]{1,0:T(8,128)(2,1)} %copy-done.2, bf16[1024,256]{1,0:T(8,128)(2,1)} %collective-permute-done.3.refs_1_, bf16[1024,256]{1,0:T(8,128)(2,1)} %copy-done.4, bf16[1024,256]{1,0:T(8,128)(2,1)} %collective-permute-done.5.refs_3_, ...), custom_call_target="tpu_custom_call" | custom-call | tf_op jit(solution)/shard_map/gather_sum/pallas_call | solution.py:272
  70.3 2.1 collective-permute-start.10
  72.4 3.2 collective-permute-start.11
  77.4 8.1 %gather_sum.13 = bf16[1024,256]{1,0:T(8,128)(2,1)} custom-call(s32[4096]{0:T(1024)} %bitcast.117, bf16[1024,256]{1,0:T(8,128)(2,1)} %copy-done.1, bf16[1024,256]{1,0:T(8,128)(2,1)} %copy-done.9, bf16[1024,256]{1,0:T(8,128)(2,1)} %copy-done.7, bf16[1024,256]{1,0:T(8,128)(2,1)} %copy-done.10, bf16[1024,256]{1,0:T(8,128)(2,1)} %copy-done.8, ...), custom_call_target="tpu_custom_call" | custom-call | tf_op jit(solution)/shard_map/gather_sum/pallas_call | solution.py:272
  85.5 2.1 collective-permute-start.20
  87.5 8.1 %gather_sum.14 = bf16[1024,256]{1,0:T(8,128)(2,1)} custom-call(s32[4096]{0:T(1024)} %bitcast.119, bf16[1024,256]{1,0:T(8,128)(2,1)} %copy-done.1, bf16[1024,256]{1,0:T(8,128)(2,1)} %copy-done.9, bf16[1024,256]{1,0:T(8,128)(2,1)} %copy-done.7, bf16[1024,256]{1,0:T(8,128)(2,1)} %copy-done.10, bf16[1024,256]{1,0:T(8,128)(2,1)} %copy-done.8, ...), custom_call_target="tpu_custom_call" | custom-call | tf_op jit(solution)/shard_map/gather_sum/pallas_call | solution.py:272
  96.9 8.1 %gather_sum.15 = bf16[1024,256]{1,0:T(8,128)(2,1)} custom-call(s32[4096]{0:T(1024)} %bitcast.121, bf16[1024,256]{1,0:T(8,128)(2,1)} %copy-done.1, bf16[1024,256]{1,0:T(8,128)(2,1)} %copy-done.9, bf16[1024,256]{1,0:T(8,128)(2,1)} %copy-done.7, bf16[1024,256]{1,0:T(8,128)(2,1)} %copy-done.10, bf16[1024,256]{1,0:T(8,128)(2,1)} %copy-done.8, ...), custom_call_target="tpu_custom_call" | custom-call | tf_op jit(solution)/shard_map/gather_sum/pallas_call | solution.py:272
  106.6 8.3 %gather_sum.12 = f32[1024,256]{1,0:T(8,128)} custom-call(s32[4096]{0:T(1024)} %bitcast.115, bf16[1024,256]{1,0:T(8,128)(2,1)} %copy-done.1, bf16[1024,256]{1,0:T(8,128)(2,1)} %copy-done.9, bf16[1024,256]{1,0:T(8,128)(2,1)} %copy-done.7, bf16[1024,256]{1,0:T(8,128)(2,1)} %copy-done.10, bf16[1024,256]{1,0:T(8,128)(2,1)} %copy-done.8, ...), custom_call_target="tpu_custom_call" | custom-call | tf_op jit(solution)/shard_map/gather_sum/pallas_call | solution.py:272
  114.9 29.8 %collective-permute-done.12 = bf16[1024,256]{1,0:T(8,128)(2,1)} collective-permute-done((bf16[1024,256]{1,0:T(8,128)(2,1)}, bf16[1024,256]{1,0:T(8,128)(2,1)}, u32[]{:S(2)}, u32[]{:S(2)}) %collective-permute-start.12) | collective-permute-done | bytes 524320 | tf_op jit(solution)/shard_map/ppermute | solution.py:343
  144.7 2.4 add_convert_fusion.7.refs_0_
  147.1 8.7 %collective-permute-done.21 = bf16[1024,256]{1,0:T(8,128)(2,1)S(1)} collective-permute-done((bf16[1024,256]{1,0:T(8,128)(2,1)}, bf16[1024,256]{1,0:T(8,128)(2,1)S(1)}, u32[]{:S(2)}, u32[]{:S(2)}) %collective-permute-start.21) | collective-permute-done | bytes 524320 | tf_op jit(solution)/shard_map/ppermute | solution.py:343
  155.8 10.4 %collective-permute-done.22 = bf16[1024,256]{1,0:T(8,128)(2,1)S(1)} collective-permute-done((bf16[1024,256]{1,0:T(8,128)(2,1)}, bf16[1024,256]{1,0:T(8,128)(2,1)S(1)}, u32[]{:S(2)}, u32[]{:S(2)}) %collective-permute-start.22) | collective-permute-done | bytes 524320 | tf_op jit(solution)/shard_map/ppermute | solution.py:343
  167.3 43.4 %dense_step.1 = (bf16[1024,256]{1,0:T(8,128)(2,1)}, bf16[1024,256]{1,0:T(8,128)(2,1)}, bf16[1024,512]{1,0:T(8,128)(2,1)}, bf16[1024,512]{1,0:T(8,128)(2,1)}, bf16[1024,2048]{1,0:T(8,128)(2,1)}) custom-call(bf16[1024,256]{1,0:T(8,128)(2,1)} %add_convert_fusion.7.refs_0_, bf16[1024,256]{1,0:T(8,128)(2,1)} %add_convert_fusion.6.refs_1_, ...), custom_call_target="tpu_custom_call" | custom-call | tf_op jit(solution)/shard_map/dense_step/pallas_call | solution.py:189
  210.7 2.1 fusion.41
  213.2 3.7 fusion.40
  217.3 2.3 copy-done
  219.8 3.1 collective-permute-done.43
  223.0 2.5 bitcast_add_fusion
  227.2 15.4 %collective-permute-done.44 = bf16[2,2,2,16,2560]{4,3,0,1,2:T(8,128)(2,1)} collective-permute-done((bf16[2,2,2,16,2560]{4,3,0,1,2:T(8,128)(2,1)S(1)}, bf16[2,2,2,16,2560]{4,3,0,1,2:T(8,128)(2,1)}, u32[]{:S(2)}, u32[]{:S(2)}) %collective-permute-start.44) | collective-permute-done | bytes 655392 | tf_op jit(solution)/shard_map/ppermute | solution.py:343
  246.4 7.4 %collective-permute-done.45 = bf16[2,2,16,2560]{3,2,0,1:T(8,128)(2,1)S(1)} collective-permute-done((bf16[2,2,16,2560]{3,2,0,1:T(8,128)(2,1)S(1)}, bf16[2,2,16,2560]{3,2,0,1:T(8,128)(2,1)S(1)}, u32[]{:S(2)}, u32[]{:S(2)}) %collective-permute-start.45) | collective-permute-done | bytes 327712 | tf_op jit(solution)/shard_map/ppermute | solution.py:343
  255.1 5.3 %collective-permute-done.46 = bf16[2,16,2560]{2,1,0:T(8,128)(2,1)S(1)} collective-permute-done((bf16[2,16,2560]{2,1,0:T(8,128)(2,1)S(1)}, bf16[2,16,2560]{2,1,0:T(8,128)(2,1)S(1)}, u32[]{:S(2)}, u32[]{:S(2)}) %collective-permute-start.46) | collective-permute-done | bytes 163872 | tf_op jit(solution)/shard_map/ppermute | solution.py:343
  260.4 2.3 collective-permute-start.47
  262.7 3.2 collective-permute-done.47
  266.8 2.2 collective-permute-start.48
  268.9 3.0 collective-permute-start.23
  273.5 2.9 collective-permute-start.49
  277.2 14.0 %collective-permute-done.23.refs_1_ = bf16[1024,256]{1,0:T(8,128)(2,1)S(1)} collective-permute-done((bf16[1024,256]{1,0:T(8,128)(2,1)S(1)}, bf16[1024,256]{1,0:T(8,128)(2,1)S(1)}, u32[]{:S(2)}, u32[]{:S(2)}) %collective-permute-start.23) | collective-permute-done | bytes 524320 | tf_op jit(solution)/shard_map/ppermute | solution.py:343
  291.2 4.0 collective-permute-start.34
  295.2 11.2 %collective-permute-done.24.refs_2_ = bf16[1024,256]{1,0:T(8,128)(2,1)S(1)} collective-permute-done((bf16[1024,256]{1,0:T(8,128)(2,1)S(1)}, bf16[1024,256]{1,0:T(8,128)(2,1)S(1)}, u32[]{:S(2)}, u32[]{:S(2)}) %collective-permute-start.24) | collective-permute-done | bytes 524320 | tf_op jit(solution)/shard_map/ppermute | solution.py:343
  306.4 1.9 collective-permute-start.35
  308.3 34.2 %collective-permute-done.25.refs_3_ = bf16[1024,256]{1,0:T(8,128)(2,1)S(1)} collective-permute-done((bf16[1024,256]{1,0:T(8,128)(2,1)S(1)}, bf16[1024,256]{1,0:T(8,128)(2,1)S(1)}, u32[]{:S(2)}, u32[]{:S(2)}) %collective-permute-start.25) | collective-permute-done | bytes 524320 | tf_op jit(solution)/shard_map/ppermute | solution.py:343
  343.2 36.7 %scatter_add.2 = (f32[1024,256]{1,0:T(8,128)}, bf16[1024,256]{1,0:T(8,128)(2,1)}, bf16[1024,256]{1,0:T(8,128)(2,1)}, bf16[1024,256]{1,0:T(8,128)(2,1)}, bf16[102...) custom-call(s32[16384]{0:T(1024)} %bitcast.112, ...), custom_call_target="tpu_custom_call" | custom-call | tf_op jit(solution)/shard_map/scatter_add/pallas_call | solution.py:323
  382.6 36.7 %scatter_add.3 = (f32[1024,256]{1,0:T(8,128)}, bf16[1024,256]{1,0:T(8,128)(2,1)}, bf16[1024,256]{1,0:T(8,128)(2,1)}, bf16[1024,256]{1,0:T(8,128)(2,1)}, bf16[102...) custom-call(s32[16384]{0:T(1024)} %bitcast.113, ...), custom_call_target="tpu_custom_call" | custom-call | tf_op jit(solution)/shard_map/scatter_add/pallas_call | solution.py:323
  424.3 14.6 %collective-permute-done.51 = bf16[8,16,2560]{2,1,0:T(8,128)(2,1)S(1)} collective-permute-done((bf16[8,16,2560]{2,1,0:T(8,128)(2,1)S(1)}, bf16[8,16,2560]{2,1,0:T(8,128)(2,1)S(1)}, u32[]{:S(2)}, u32[]{:S(2)}) %collective-permute-start.51) | collective-permute-done | bytes 655392 | tf_op jit(solution)/shard_map/ppermute | solution.py:343
  439.8 2.6 collective-permute-start.32
  444.8 5.4 %collective-permute-done.28 = bf16[1024,256]{1,0:T(8,128)(2,1)S(1)} collective-permute-done((bf16[1024,256]{1,0:T(8,128)(2,1)S(1)}, bf16[1024,256]{1,0:T(8,128)(2,1)S(1)}, u32[]{:S(2)}, u32[]{:S(2)}) %collective-permute-start.28) | collective-permute-done | bytes 524320 | tf_op jit(solution)/shard_map/ppermute | solution.py:343
  451.7 13.1 %collective-permute-done.30 = bf16[1024,256]{1,0:T(8,128)(2,1)S(1)} collective-permute-done((bf16[1024,256]{1,0:T(8,128)(2,1)S(1)}, bf16[1024,256]{1,0:T(8,128)(2,1)S(1)}, u32[]{:S(2)}, u32[]{:S(2)}) %collective-permute-start.30) | collective-permute-done | bytes 524320 | tf_op jit(solution)/shard_map/ppermute | solution.py:343
  466.4 2.2 collective-permute-start.42
  468.6 2.2 convert_add_fusion.1
  470.8 2.0 collective-permute-done.38
  472.8 12.8 %collective-permute-done.40 = bf16[1024,256]{1,0:T(8,128)(2,1)} collective-permute-done((bf16[1024,256]{1,0:T(8,128)(2,1)}, bf16[1024,256]{1,0:T(8,128)(2,1)}, u32[]{:S(2)}, u32[]{:S(2)}) %collective-permute-start.40) | collective-permute-done | bytes 524320 | tf_op jit(solution)/shard_map/ppermute | solution.py:343
  (206 shorter events, 54.5 us)
Async XLA Ops:
  2.0 14.9 %collective-permute-start.4 = (bf16[1024,256]{1,0:T(8,128)(2,1)S(1)}, bf16[1024,256]{1,0:T(8,128)(2,1)S(1)}, u32[]{:S(2)}, u32[]{:S(2)}) collective-permute-start(bf16[1024,256]{1,0:T(8,128)(2,1)S(1)} %get-tuple-element.77.refs_0_), channel_id=1, source_target_pairs={{0,2},{1,3},{2,0},{3,1},{4,6},{5,7},{6,4},{7,5},{8,10},{9,11},{10,... | collective-permute-start | bytes 1572872 | tf_op jit(solution)/shard_map/ppermute | solution.py:343
  3.5 27.1 %collective-permute-start.6 = (bf16[1024,256]{1,0:T(8,128)(2,1)S(1)}, bf16[1024,256]{1,0:T(8,128)(2,1)S(1)}, u32[]{:S(2)}, u32[]{:S(2)}) collective-permute-start(bf16[1024,256]{1,0:T(8,128)(2,1)S(1)} %get-tuple-element.77.refs_0_), channel_id=1, source_target_pairs={{0,4},{1,5},{2,6},{3,7},{4,0},{5,1},{6,2},{7,3},{8,12},{9,13},{10,... | collective-permute-start | bytes 1572872 | tf_op jit(solution)/shard_map/ppermute | solution.py:343
  5.0 27.1 %collective-permute-start.8 = (bf16[1024,256]{1,0:T(8,128)(2,1)S(1)}, bf16[1024,256]{1,0:T(8,128)(2,1)S(1)}, u32[]{:S(2)}, u32[]{:S(2)}) collective-permute-start(bf16[1024,256]{1,0:T(8,128)(2,1)S(1)} %get-tuple-element.77.refs_0_), channel_id=1, source_target_pairs={{0,6},{1,7},{2,4},{3,5},{4,2},{5,3},{6,0},{7,1},{8,14},{9,15},{10,... | collective-permute-start | bytes 1572872 | tf_op jit(solution)/shard_map/ppermute | solution.py:343
  5.5 27.1 %collective-permute-start.3 = (bf16[1024,256]{1,0:T(8,128)(2,1)S(1)}, bf16[1024,256]{1,0:T(8,128)(2,1)}, u32[]{:S(2)}, u32[]{:S(2)}) collective-permute-start(bf16[1024,256]{1,0:T(8,128)(2,1)S(1)} %get-tuple-element.77.refs_0_), channel_id=1, source_target_pairs={{0,1},{1,0},{2,3},{3,2},{4,5},{5,4},{6,7},{7,6},{8,9},{9,8},{10,11... | collective-permute-start | bytes 1572872 | tf_op jit(solution)/shard_map/ppermute | solution.py:343
  16.8 15.8 %collective-permute-start.5 = (bf16[1024,256]{1,0:T(8,128)(2,1)S(1)}, bf16[1024,256]{1,0:T(8,128)(2,1)}, u32[]{:S(2)}, u32[]{:S(2)}) collective-permute-start(bf16[1024,256]{1,0:T(8,128)(2,1)S(1)} %collective-permute-done.4.refs_2_), channel_id=1, source_target_pairs={{0,1},{1,0},{2,3},{3,2},{4,5},{5,4},{6,7},{7,6},{8,9},{9,8},{10,11... | collective-permute-start | bytes 1572872 | tf_op jit(solution)/shard_map/ppermute | solution.py:343
  16.9 3.8 collective-permute-start
  20.7 4.6 collective-permute-start.1
  29.1 40.1 %collective-permute-start.13 = (bf16[1024,256]{1,0:T(8,128)(2,1)S(1)}, bf16[1024,256]{1,0:T(8,128)(2,1)S(1)}, u32[]{:S(2)}, u32[]{:S(2)}) collective-permute-start(bf16[1024,256]{1,0:T(8,128)(2,1)S(1)} %get-tuple-element.30.refs_0_), channel_id=1, source_target_pairs={{0,2},{1,3},{2,0},{3,1},{4,6},{5,7},{6,4},{7,5},{8,10},{9,11},{10,... | collective-permute-start | bytes 1572872 | tf_op jit(solution)/shard_map/ppermute | solution.py:343
  30.6 38.6 %collective-permute-start.14 = (bf16[1024,256]{1,0:T(8,128)(2,1)S(1)}, bf16[1024,256]{1,0:T(8,128)(2,1)S(1)}, u32[]{:S(2)}, u32[]{:S(2)}) collective-permute-start(bf16[1024,256]{1,0:T(8,128)(2,1)S(1)} %get-tuple-element.30.refs_0_), channel_id=1, source_target_pairs={{0,4},{1,5},{2,6},{3,7},{4,0},{5,1},{6,2},{7,3},{8,12},{9,13},{10,... | collective-permute-start | bytes 1572872 | tf_op jit(solution)/shard_map/ppermute | solution.py:343
  32.1 37.1 %collective-permute-start.15 = (bf16[1024,256]{1,0:T(8,128)(2,1)S(1)}, bf16[1024,256]{1,0:T(8,128)(2,1)}, u32[]{:S(2)}, u32[]{:S(2)}) collective-permute-start(bf16[1024,256]{1,0:T(8,128)(2,1)S(1)} %get-tuple-element.30.refs_0_), channel_id=1, source_target_pairs={{0,6},{1,7},{2,4},{3,5},{4,2},{5,3},{6,0},{7,1},{8,14},{9,15},{10,... | collective-permute-start | bytes 1572872 | tf_op jit(solution)/shard_map/ppermute | solution.py:343
  69.3 6.3 %collective-permute-start.17 = (bf16[1024,256]{1,0:T(8,128)(2,1)S(1)}, bf16[1024,256]{1,0:T(8,128)(2,1)S(1)}, u32[]{:S(2)}, u32[]{:S(2)}) collective-permute-start(bf16[1024,256]{1,0:T(8,128)(2,1)S(1)} %collective-permute-done.13.refs_2_), channel_id=1, source_target_pairs={{0,1},{1,0},{2,3},{3,2},{4,5},{5,4},{6,7},{7,6},{8,9},{9,8},{10,11... | collective-permute-start | bytes 1572872 | tf_op jit(solution)/shard_map/ppermute | solution.py:343
  69.8 5.9 %collective-permute-start.18 = (bf16[1024,256]{1,0:T(8,128)(2,1)S(1)}, bf16[1024,256]{1,0:T(8,128)(2,1)S(1)}, u32[]{:S(2)}, u32[]{:S(2)}) collective-permute-start(bf16[1024,256]{1,0:T(8,128)(2,1)S(1)} %collective-permute-done.14.refs_4_), channel_id=1, source_target_pairs={{0,1},{1,0},{2,3},{3,2},{4,5},{5,4},{6,7},{7,6},{8,9},{9,8},{10,11... | collective-permute-start | bytes 1572872 | tf_op jit(solution)/shard_map/ppermute | solution.py:343
  69.9 5.8 %collective-permute-start.19 = (bf16[1024,256]{1,0:T(8,128)(2,1)}, bf16[1024,256]{1,0:T(8,128)(2,1)S(1)}, u32[]{:S(2)}, u32[]{:S(2)}) collective-permute-start(bf16[1024,256]{1,0:T(8,128)(2,1)} %collective-permute-done.15.refs_6_), channel_id=1, source_target_pairs={{0,1},{1,0},{2,3},{3,2},{4,5},{5,4},{6,7},{7,6},{8,9},{9,8},{10,11... | collective-permute-start | bytes 1572872 | tf_op jit(solution)/shard_map/ppermute | solution.py:343
  70.3 34.7 %collective-permute-start.10 = (bf16[1024,256]{1,0:T(8,128)(2,1)}, bf16[1024,256]{1,0:T(8,128)(2,1)}, u32[]{:S(2)}, u32[]{:S(2)}) collective-permute-start(bf16[1024,256]{1,0:T(8,128)(2,1)} %gather_sum.9), channel_id=1, source_target_pairs={{0,8},{1,9},{2,10},{3,11},{4,12},{5,13},{6,14},{7,15},{8,0},{9,1},... | collective-permute-start | bytes 1572872 | tf_op jit(solution)/shard_map/ppermute | solution.py:343
  72.4 42.5 %collective-permute-start.11 = (bf16[1024,256]{1,0:T(8,128)(2,1)}, bf16[1024,256]{1,0:T(8,128)(2,1)}, u32[]{:S(2)}, u32[]{:S(2)}) collective-permute-start(bf16[1024,256]{1,0:T(8,128)(2,1)} %gather_sum.10), channel_id=1, source_target_pairs={{0,16},{1,17},{2,18},{3,19},{4,20},{5,21},{6,22},{7,23},{8,24},{9,... | collective-permute-start | bytes 1572872 | tf_op jit(solution)/shard_map/ppermute | solution.py:343
  75.6 69.0 %collective-permute-start.12 = (bf16[1024,256]{1,0:T(8,128)(2,1)}, bf16[1024,256]{1,0:T(8,128)(2,1)}, u32[]{:S(2)}, u32[]{:S(2)}) collective-permute-start(bf16[1024,256]{1,0:T(8,128)(2,1)} %gather_sum.11), channel_id=1, source_target_pairs={{0,24},{1,25},{2,26},{3,27},{4,28},{5,29},{6,30},{7,31},{8,16},{9,... | collective-permute-start | bytes 1572872 | tf_op jit(solution)/shard_map/ppermute | solution.py:343
  85.5 61.6 %collective-permute-start.20 = (bf16[1024,256]{1,0:T(8,128)(2,1)}, bf16[1024,256]{1,0:T(8,128)(2,1)S(1)}, u32[]{:S(2)}, u32[]{:S(2)}) collective-permute-start(bf16[1024,256]{1,0:T(8,128)(2,1)} %gather_sum.13), channel_id=1, source_target_pairs={{0,8},{1,9},{2,10},{3,11},{4,12},{5,13},{6,14},{7,15},{8,0},{9,1},... | collective-permute-start | bytes 1572872 | tf_op jit(solution)/shard_map/ppermute | solution.py:343
  95.6 60.2 %collective-permute-start.21 = (bf16[1024,256]{1,0:T(8,128)(2,1)}, bf16[1024,256]{1,0:T(8,128)(2,1)S(1)}, u32[]{:S(2)}, u32[]{:S(2)}) collective-permute-start(bf16[1024,256]{1,0:T(8,128)(2,1)} %gather_sum.14), channel_id=1, source_target_pairs={{0,16},{1,17},{2,18},{3,19},{4,20},{5,21},{6,22},{7,23},{8,24},{9,... | collective-permute-start | bytes 1572872 | tf_op jit(solution)/shard_map/ppermute | solution.py:343
  105.0 61.2 %collective-permute-start.22 = (bf16[1024,256]{1,0:T(8,128)(2,1)}, bf16[1024,256]{1,0:T(8,128)(2,1)S(1)}, u32[]{:S(2)}, u32[]{:S(2)}) collective-permute-start(bf16[1024,256]{1,0:T(8,128)(2,1)} %gather_sum.15), channel_id=1, source_target_pairs={{0,24},{1,25},{2,26},{3,27},{4,28},{5,29},{6,30},{7,31},{8,16},{9,... | collective-permute-start | bytes 1572872 | tf_op jit(solution)/shard_map/ppermute | solution.py:343
  225.6 16.9 %collective-permute-start.44 = (bf16[2,2,2,16,2560]{4,3,0,1,2:T(8,128)(2,1)S(1)}, bf16[2,2,2,16,2560]{4,3,0,1,2:T(8,128)(2,1)}, u32[]{:S(2)}, u32[]{:S(2)}) collective-permute-start(bf16[2,2,2,16,2560]{4,3,0,1,2:T(8,128)(2,1)S(1)} %fusion.1), channel_id=1, source_target_pairs={{0,2},{1,3},{2,0},{3,1},{4,6},{5,7},{6,4},{7,5},{8,10},{9,11},{10,... | collective-permute-start | bytes 1966088 | tf_op jit(solution)/shard_map/ppermute | solution.py:343
  244.8 9.0 %collective-permute-start.45 = (bf16[2,2,16,2560]{3,2,0,1:T(8,128)(2,1)S(1)}, bf16[2,2,16,2560]{3,2,0,1:T(8,128)(2,1)S(1)}, u32[]{:S(2)}, u32[]{:S(2)}) collective-permute-start(bf16[2,2,16,2560]{3,2,0,1:T(8,128)(2,1)S(1)} %fusion.2), channel_id=1, source_target_pairs={{0,4},{1,5},{2,6},{3,7},{4,0},{5,1},{6,2},{7,3},{8,12},{9,13},{10,... | collective-permute-start | bytes 983048 | tf_op jit(solution)/shard_map/ppermute | solution.py:343
  255.0 5.4 %collective-permute-start.46 = (bf16[2,16,2560]{2,1,0:T(8,128)(2,1)S(1)}, bf16[2,16,2560]{2,1,0:T(8,128)(2,1)S(1)}, u32[]{:S(2)}, u32[]{:S(2)}) collective-permute-start(bf16[2,16,2560]{2,1,0:T(8,128)(2,1)S(1)} %fusion.4), channel_id=1, source_target_pairs={{0,8},{1,9},{2,10},{3,11},{4,12},{5,13},{6,14},{7,15},{8,0},{9,1},... | collective-permute-start | bytes 491528 | tf_op jit(solution)/shard_map/ppermute | solution.py:343
  260.4 5.5 %collective-permute-start.47 = (bf16[16,2560]{1,0:T(8,128)(2,1)S(1)}, bf16[16,2560]{1,0:T(8,128)(2,1)S(1)}, u32[]{:S(2)}, u32[]{:S(2)}) collective-permute-start(bf16[16,2560]{1,0:T(8,128)(2,1)S(1)} %fusion.5), channel_id=1, source_target_pairs={{0,16},{1,17},{2,18},{3,19},{4,20},{5,21},{6,22},{7,23},{8,24},{9,... | collective-permute-start | bytes 245768 | tf_op jit(solution)/shard_map/ppermute | solution.py:343
  266.8 6.7 %collective-permute-start.48 = (bf16[1,16,2560]{2,1,0:T(8,128)(2,1)S(1)}, bf16[1,16,2560]{2,1,0:T(8,128)(2,1)S(1)}, u32[]{:S(2)}, u32[]{:S(2)}) collective-permute-start(bf16[1,16,2560]{2,1,0:T(8,128)(2,1)S(1)} %get-tuple-element.55), channel_id=1, source_target_pairs={{0,16},{1,17},{2,18},{3,19},{4,20},{5,21},{6,22},{7,23},{8,24},{9,... | collective-permute-start | bytes 245768 | tf_op jit(solution)/shard_map/ppermute | solution.py:343
  268.9 22.3 %collective-permute-start.23 = (bf16[1024,256]{1,0:T(8,128)(2,1)S(1)}, bf16[1024,256]{1,0:T(8,128)(2,1)S(1)}, u32[]{:S(2)}, u32[]{:S(2)}) collective-permute-start(bf16[1024,256]{1,0:T(8,128)(2,1)S(1)} %copy-done.27), channel_id=1, source_target_pairs={{0,8},{1,9},{2,10},{3,11},{4,12},{5,13},{6,14},{7,15},{8,0},{9,1},... | collective-permute-start | bytes 1572872 | tf_op jit(solution)/shard_map/ppermute | solution.py:343
  271.9 34.5 %collective-permute-start.24 = (bf16[1024,256]{1,0:T(8,128)(2,1)S(1)}, bf16[1024,256]{1,0:T(8,128)(2,1)S(1)}, u32[]{:S(2)}, u32[]{:S(2)}) collective-permute-start(bf16[1024,256]{1,0:T(8,128)(2,1)S(1)} %copy-done.27), channel_id=1, source_target_pairs={{0,16},{1,17},{2,18},{3,19},{4,20},{5,21},{6,22},{7,23},{8,24},{9,... | collective-permute-start | bytes 1572872 | tf_op jit(solution)/shard_map/ppermute | solution.py:343
  272.1 70.3 %collective-permute-start.25 = (bf16[1024,256]{1,0:T(8,128)(2,1)S(1)}, bf16[1024,256]{1,0:T(8,128)(2,1)S(1)}, u32[]{:S(2)}, u32[]{:S(2)}) collective-permute-start(bf16[1024,256]{1,0:T(8,128)(2,1)S(1)} %copy-done.27), channel_id=1, source_target_pairs={{0,24},{1,25},{2,26},{3,27},{4,28},{5,29},{6,30},{7,31},{8,16},{9,... | collective-permute-start | bytes 1572872 | tf_op jit(solution)/shard_map/ppermute | solution.py:343
  273.5 106.5 %collective-permute-start.49 = (bf16[2,16,2560]{2,1,0:T(8,128)(2,1)S(1)}, bf16[2,16,2560]{2,1,0:T(8,128)(2,1)S(1)}, u32[]{:S(2)}, u32[]{:S(2)}) collective-permute-start(bf16[2,16,2560]{2,1,0:T(8,128)(2,1)S(1)} %maximum_bitcast_fusion), channel_id=1, source_target_pairs={{0,8},{1,9},{2,10},{3,11},{4,12},{5,13},{6,14},{7,15},{8,0},{9,1},... | collective-permute-start | bytes 491528 | tf_op jit(solution)/shard_map/ppermute | solution.py:343
  277.1 104.5 %collective-permute-start.33 = (bf16[1024,256]{1,0:T(8,128)(2,1)S(1)}, bf16[1024,256]{1,0:T(8,128)(2,1)S(1)}, u32[]{:S(2)}, u32[]{:S(2)}) collective-permute-start(bf16[1024,256]{1,0:T(8,128)(2,1)S(1)} %copy-done.26), channel_id=1, source_target_pairs={{0,8},{1,9},{2,10},{3,11},{4,12},{5,13},{6,14},{7,15},{8,0},{9,1},... | collective-permute-start | bytes 1572872 | tf_op jit(solution)/shard_map/ppermute | solution.py:343
  291.2 90.7 %collective-permute-start.34 = (bf16[1024,256]{1,0:T(8,128)(2,1)S(1)}, bf16[1024,256]{1,0:T(8,128)(2,1)S(1)}, u32[]{:S(2)}, u32[]{:S(2)}) collective-permute-start(bf16[1024,256]{1,0:T(8,128)(2,1)S(1)} %copy-done.26), channel_id=1, source_target_pairs={{0,16},{1,17},{2,18},{3,19},{4,20},{5,21},{6,22},{7,23},{8,24},{9,... | collective-permute-start | bytes 1572872 | tf_op jit(solution)/shard_map/ppermute | solution.py:343
  306.4 75.8 %collective-permute-start.35 = (bf16[1024,256]{1,0:T(8,128)(2,1)S(1)}, bf16[1024,256]{1,0:T(8,128)(2,1)}, u32[]{:S(2)}, u32[]{:S(2)}) collective-permute-start(bf16[1024,256]{1,0:T(8,128)(2,1)S(1)} %copy-done.26), channel_id=1, source_target_pairs={{0,24},{1,25},{2,26},{3,27},{4,28},{5,29},{6,30},{7,31},{8,16},{9,... | collective-permute-start | bytes 1572872 | tf_op jit(solution)/shard_map/ppermute | solution.py:343
  379.9 39.4 %collective-permute-start.27 = (bf16[1024,256]{1,0:T(8,128)(2,1)}, bf16[1024,256]{1,0:T(8,128)(2,1)S(1)}, u32[]{:S(2)}, u32[]{:S(2)}) collective-permute-start(bf16[1024,256]{1,0:T(8,128)(2,1)} %get-tuple-element.38), channel_id=1, source_target_pairs={{0,1},{1,0},{2,3},{3,2},{4,5},{5,4},{6,7},{7,6},{8,9},{9,8},{10,11... | collective-permute-start | bytes 1572872 | tf_op jit(solution)/shard_map/ppermute | solution.py:343
  380.0 39.7 %collective-permute-start.50 = (bf16[4,16,2560]{2,1,0:T(8,128)(2,1)S(1)}, bf16[4,16,2560]{2,1,0:T(8,128)(2,1)}, u32[]{:S(2)}, u32[]{:S(2)}) collective-permute-start(bf16[4,16,2560]{2,1,0:T(8,128)(2,1)S(1)} %bitcast.111), channel_id=1, source_target_pairs={{0,4},{1,5},{2,6},{3,7},{4,0},{5,1},{6,2},{7,3},{8,12},{9,13},{10,... | collective-permute-start | bytes 983048 | tf_op jit(solution)/shard_map/ppermute | solution.py:343
  381.6 39.6 %collective-permute-start.29 = (bf16[1024,256]{1,0:T(8,128)(2,1)}, bf16[1024,256]{1,0:T(8,128)(2,1)S(1)}, u32[]{:S(2)}, u32[]{:S(2)}) collective-permute-start(bf16[1024,256]{1,0:T(8,128)(2,1)} %get-tuple-element.40), channel_id=1, source_target_pairs={{0,1},{1,0},{2,3},{3,2},{4,5},{5,4},{6,7},{7,6},{8,9},{9,8},{10,11... | collective-permute-start | bytes 1572872 | tf_op jit(solution)/shard_map/ppermute | solution.py:343
  381.9 41.1 %collective-permute-start.31 = (bf16[1024,256]{1,0:T(8,128)(2,1)}, bf16[1024,256]{1,0:T(8,128)(2,1)S(1)}, u32[]{:S(2)}, u32[]{:S(2)}) collective-permute-start(bf16[1024,256]{1,0:T(8,128)(2,1)} %get-tuple-element.42), channel_id=1, source_target_pairs={{0,1},{1,0},{2,3},{3,2},{4,5},{5,4},{6,7},{7,6},{8,9},{9,8},{10,11... | collective-permute-start | bytes 1572872 | tf_op jit(solution)/shard_map/ppermute | solution.py:343
  382.2 62.1 %collective-permute-start.26 = (bf16[1024,256]{1,0:T(8,128)(2,1)}, bf16[1024,256]{1,0:T(8,128)(2,1)}, u32[]{:S(2)}, u32[]{:S(2)}) collective-permute-start(bf16[1024,256]{1,0:T(8,128)(2,1)} %get-tuple-element.36), channel_id=1, source_target_pairs={{0,1},{1,0},{2,3},{3,2},{4,5},{5,4},{6,7},{7,6},{8,9},{9,8},{10,11... | collective-permute-start | bytes 1572872 | tf_op jit(solution)/shard_map/ppermute | solution.py:343
  419.3 3.9 collective-permute-start.37
  419.8 20.0 %collective-permute-start.39 = (bf16[1024,256]{1,0:T(8,128)(2,1)}, bf16[1024,256]{1,0:T(8,128)(2,1)S(1)}, u32[]{:S(2)}, u32[]{:S(2)}) collective-permute-start(bf16[1024,256]{1,0:T(8,128)(2,1)} %get-tuple-element.49), channel_id=1, source_target_pairs={{0,1},{1,0},{2,3},{3,2},{4,5},{5,4},{6,7},{7,6},{8,9},{9,8},{10,11... | collective-permute-start | bytes 1572872 | tf_op jit(solution)/shard_map/ppermute | solution.py:343
  421.2 17.7 %collective-permute-start.51 = (bf16[8,16,2560]{2,1,0:T(8,128)(2,1)S(1)}, bf16[8,16,2560]{2,1,0:T(8,128)(2,1)S(1)}, u32[]{:S(2)}, u32[]{:S(2)}) collective-permute-start(bf16[8,16,2560]{2,1,0:T(8,128)(2,1)S(1)} %bitcast.110), channel_id=1, source_target_pairs={{0,2},{1,3},{2,0},{3,1},{4,6},{5,7},{6,4},{7,5},{8,10},{9,11},{10,... | collective-permute-start | bytes 1966088 | tf_op jit(solution)/shard_map/ppermute | solution.py:343
  423.0 19.4 %collective-permute-start.41 = (bf16[1024,256]{1,0:T(8,128)(2,1)S(1)}, bf16[1024,256]{1,0:T(8,128)(2,1)S(1)}, u32[]{:S(2)}, u32[]{:S(2)}) collective-permute-start(bf16[1024,256]{1,0:T(8,128)(2,1)S(1)} %copy-done.42), channel_id=1, source_target_pairs={{0,1},{1,0},{2,3},{3,2},{4,5},{5,4},{6,7},{7,6},{8,9},{9,8},{10,11... | collective-permute-start | bytes 1572872 | tf_op jit(solution)/shard_map/ppermute | solution.py:343
  423.2 26.9 %collective-permute-start.28 = (bf16[1024,256]{1,0:T(8,128)(2,1)S(1)}, bf16[1024,256]{1,0:T(8,128)(2,1)S(1)}, u32[]{:S(2)}, u32[]{:S(2)}) collective-permute-start(bf16[1024,256]{1,0:T(8,128)(2,1)S(1)} %add_convert_fusion.5), channel_id=1, source_target_pairs={{0,2},{1,3},{2,0},{3,1},{4,6},{5,7},{6,4},{7,5},{8,10},{9,11},{10,... | collective-permute-start | bytes 1572872 | tf_op jit(solution)/shard_map/ppermute | solution.py:343
  438.9 25.9 %collective-permute-start.30 = (bf16[1024,256]{1,0:T(8,128)(2,1)S(1)}, bf16[1024,256]{1,0:T(8,128)(2,1)S(1)}, u32[]{:S(2)}, u32[]{:S(2)}) collective-permute-start(bf16[1024,256]{1,0:T(8,128)(2,1)S(1)} %add_convert_fusion.4), channel_id=1, source_target_pairs={{0,4},{1,5},{2,6},{3,7},{4,0},{5,1},{6,2},{7,3},{8,12},{9,13},{10,... | collective-permute-start | bytes 1572872 | tf_op jit(solution)/shard_map/ppermute | solution.py:343
  439.8 25.0 %collective-permute-start.32 = (bf16[1024,256]{1,0:T(8,128)(2,1)S(1)}, bf16[1024,256]{1,0:T(8,128)(2,1)S(1)}, u32[]{:S(2)}, u32[]{:S(2)}) collective-permute-start(bf16[1024,256]{1,0:T(8,128)(2,1)S(1)} %add_convert_fusion.3), channel_id=1, source_target_pairs={{0,6},{1,7},{2,4},{3,5},{4,2},{5,3},{6,0},{7,1},{8,14},{9,15},{10,... | collective-permute-start | bytes 1572872 | tf_op jit(solution)/shard_map/ppermute | solution.py:343
  442.3 46.7 %collective-permute-start.52 = (bf16[16,16,2560]{2,1,0:T(8,128)(2,1)S(1)}, bf16[16,16,2560]{2,1,0:T(8,128)(2,1)S(1)}, u32[]{:S(2)}, u32[]{:S(2)}) collective-permute-start(bf16[16,16,2560]{2,1,0:T(8,128)(2,1)S(1)} %bitcast.108), channel_id=1, source_target_pairs={{0,1},{1,0},{2,3},{3,2},{4,5},{5,4},{6,7},{7,6},{8,9},{9,8},{10,11... | collective-permute-start | bytes 3932168 | tf_op jit(solution)/shard_map/ppermute | solution.py:343
  444.2 26.5 %collective-permute-start.36 = (bf16[1024,256]{1,0:T(8,128)(2,1)}, bf16[1024,256]{1,0:T(8,128)(2,1)}, u32[]{:S(2)}, u32[]{:S(2)}) collective-permute-start(bf16[1024,256]{1,0:T(8,128)(2,1)} %get-tuple-element.45), channel_id=1, source_target_pairs={{0,1},{1,0},{2,3},{3,2},{4,5},{5,4},{6,7},{7,6},{8,9},{9,8},{10,11... | collective-permute-start | bytes 1572872 | tf_op jit(solution)/shard_map/ppermute | solution.py:343
  450.2 22.6 %collective-permute-start.38 = (bf16[1024,256]{1,0:T(8,128)(2,1)S(1)}, bf16[1024,256]{1,0:T(8,128)(2,1)}, u32[]{:S(2)}, u32[]{:S(2)}) collective-permute-start(bf16[1024,256]{1,0:T(8,128)(2,1)S(1)} %add_convert_fusion.2), channel_id=1, source_target_pairs={{0,2},{1,3},{2,0},{3,1},{4,6},{5,7},{6,4},{7,5},{8,10},{9,11},{10,... | collective-permute-start | bytes 1572872 | tf_op jit(solution)/shard_map/ppermute | solution.py:343
  464.8 20.7 %collective-permute-start.40 = (bf16[1024,256]{1,0:T(8,128)(2,1)}, bf16[1024,256]{1,0:T(8,128)(2,1)}, u32[]{:S(2)}, u32[]{:S(2)}) collective-permute-start(bf16[1024,256]{1,0:T(8,128)(2,1)} %add_convert_fusion.1), channel_id=1, source_target_pairs={{0,4},{1,5},{2,6},{3,7},{4,0},{5,1},{6,2},{7,3},{8,12},{9,13},{10,... | collective-permute-start | bytes 1572872 | tf_op jit(solution)/shard_map/ppermute | solution.py:343
  466.4 19.1 %collective-permute-start.42 = (bf16[1024,256]{1,0:T(8,128)(2,1)}, bf16[1024,256]{1,0:T(8,128)(2,1)}, u32[]{:S(2)}, u32[]{:S(2)}) collective-permute-start(bf16[1024,256]{1,0:T(8,128)(2,1)} %add_convert_fusion), channel_id=1, source_target_pairs={{0,6},{1,7},{2,4},{3,5},{4,2},{5,3},{6,0},{7,1},{8,14},{9,15},{10,... | collective-permute-start | bytes 1572872 | tf_op jit(solution)/shard_map/ppermute | solution.py:343
  (48 other events, 638.3 us)

commit v2 on v1

--- a/solution.py
+++ b/solution.py
@@ -227,53 +227,56 @@
     lax.fori_loop(0, rows // chunk, step, 0)
 
 
-def join_rows(dst, src, base, chunk):
+def join_rows(dst, srcs, base, chunk):
     rows, width = dst.shape
     parts = width // LANES
 
     def step(i, c):
         for j in range(parts):
             start = pl.multiple_of(base * parts + i * (chunk * parts), 8) + j
-            piece = src[pl.ds(start, chunk, stride=parts), :]
+            piece = srcs[0][pl.ds(start, chunk, stride=parts), :]
+            for src in srcs[1:]:
+                piece = piece + src[pl.ds(start, chunk, stride=parts), :]
             dst[pl.ds(pl.multiple_of(i * chunk, chunk), chunk), j * LANES:(j + 1) * LANES] = piece.astype(dst.dtype)
         return c
 
     lax.fori_loop(0, rows // chunk, step, 0)
 
 
-def gather_body(ntab, unroll, idx, *refs):
-    tabs, out, tab, acc = refs[:ntab], refs[ntab], refs[ntab + 1], refs[ntab + 2]
+def gather_body(ntab, nout, unroll, idx, *refs):
+    tabs, outs, tab, acc = refs[:ntab], refs[ntab:ntab + nout], refs[-2], refs[-1]
     rows, width = tabs[0].shape
     parts = width // LANES
-    count = out.shape[0]
-    feats = idx.shape[0] // count
+    count = outs[0].shape[0]
+    feats = idx.shape[0] // (count * nout)
     chunk = 64
     for i in range(ntab):
         spread_rows(tab, i * rows, tabs[i], chunk)
     tab[pl.ds(ntab * rows * parts, 8), :] = jnp.zeros((8, LANES), F32)
-
-    def step(i, c):
-        for u in range(unroll):
-            t = i * unroll + u
-            total = tab[pl.ds(idx[t], parts), :]
-            for f in range(1, feats):
-                total = total + tab[pl.ds(idx[f * count + t], parts), :]
-            acc[pl.ds(t * parts, parts), :] = total
-        return c
-
-    lax.fori_loop(0, count // unroll, step, 0)
-    join_rows(out, acc, 0, chunk)
-
-
-def gather_sum(idx, tabs, dtype, count):
+    for n, out in enumerate(outs):
+
+        def step(i, c):
+            for u in range(unroll):
+                t = i * unroll + u
+                total = tab[pl.ds(idx[n * feats * count + t], parts), :]
+                for f in range(1, feats):
+                    total = total + tab[pl.ds(idx[(n * feats + f) * count + t], parts), :]
+                acc[pl.ds(t * parts, parts), :] = total
+            return c
+
+        lax.fori_loop(0, count // unroll, step, 0)
+        join_rows(out, [acc], 0, chunk)
+
+
+def gather_sum(idx, tabs, dtypes, count):
     rows, width = tabs[0].shape
     parts = width // LANES
     vm = pl.BlockSpec(memory_space=pltpu.VMEM)
     return pl.pallas_call(
-        functools.partial(gather_body, len(tabs), 8),
-        out_shape=jax.ShapeDtypeStruct((count, width), dtype),
+        functools.partial(gather_body, len(tabs), len(dtypes), 8),
+        out_shape=tuple(jax.ShapeDtypeStruct((count, width), d) for d in dtypes),
         in_specs=[pl.BlockSpec(memory_space=pltpu.SMEM)] + [vm] * len(tabs),
-        out_specs=vm,
+        out_specs=(vm,) * len(dtypes),
         scratch_shapes=[
             pltpu.VMEM((len(tabs) * rows * parts + 8, LANES), F32),
             pltpu.VMEM((count * parts, LANES), F32),
@@ -283,8 +286,9 @@
     )(idx, *tabs)
 
 
-def scatter_body(npiece, nout, unroll, idx, *refs):
-    pieces, outs, acc, stage = refs[:npiece], refs[npiece:npiece + nout], refs[-2], refs[-1]
+def scatter_body(npiece, nout, lots, idx, *refs):
+    pieces, outs = refs[:npiece], refs[npiece:npiece + nout]
+    accs, stage = refs[npiece + nout:-1], refs[-1]
     count, width = pieces[0].shape
     rows = outs[0].shape[0]
     parts = width // LANES
@@ -292,48 +296,76 @@
     chunk = 64
 
     def clear(i, c):
-        acc[pl.ds(pl.multiple_of(i * 256, 256), 256), :] = jnp.zeros((256, LANES), F32)
+        for acc in accs:
+            acc[pl.ds(pl.multiple_of(i * 256, 256), 256), :] = jnp.zeros((256, LANES), F32)
         return c
 
     lax.fori_loop(0, nout * rows * parts // 256, clear, 0)
-    acc[pl.ds(nout * rows * parts, parts * feats), :] = jnp.zeros((parts * feats, LANES), F32)
+    for acc in accs:
+        acc[pl.ds(nout * rows * parts, parts * feats), :] = jnp.zeros((parts * feats, LANES), F32)
     for n in range(npiece):
         spread_rows(stage, 0, pieces[n], chunk)
 
         def step(i, c):
-            for u in range(unroll):
-                t = i * unroll + u
-                val = stage[pl.ds(t * parts, parts), :]
-                at = [idx[(n * feats + f) * count + t] for f in range(feats)]
-                got = [acc[pl.ds(a, parts), :] for a in at]
-                for a, g in zip(at, got):
-                    acc[pl.ds(a, parts), :] = g + val
+            for w in range(2):
+                base = (i * 2 + w) * lots
+                todo = []
+                for u, acc in enumerate(accs):
+                    val = stage[pl.ds((base + u) * parts, parts), :]
+                    for f in range(feats):
+                        at = idx[(n * feats + f) * count + base + u]
+                        todo.append((acc, at, acc[pl.ds(at, parts), :] + val))
+                for acc, at, val in todo:
+                    acc[pl.ds(at, parts), :] = val
             return c
 
-        lax.fori_loop(0, count // unroll, step, 0)
+        lax.fori_loop(0, count // (2 * lots), step, 0)
     for o in range(nout):
-        join_rows(outs[o], acc, o * rows, chunk)
+        join_rows(outs[o], accs, o * rows, chunk)
 
 
 def scatter_add(idx, pieces, nout, rows, dtypes):
     count, width = pieces[0].shape
     feats = idx.shape[0] // (len(pieces) * count)
     parts = width // LANES
+    lots = 4
     vm = pl.BlockSpec(memory_space=pltpu.VMEM)
     return pl.pallas_call(
-        functools.partial(scatter_body, len(pieces), nout, 4),
+        functools.partial(scatter_body, len(pieces), nout, lots),
         out_shape=tuple(jax.ShapeDtypeStruct((rows, width), d) for d in dtypes),
         in_specs=[pl.BlockSpec(memory_space=pltpu.SMEM)] + [vm] * len(pieces),
         out_specs=(vm,) * nout,
-        scratch_shapes=[
-            pltpu.VMEM(((nout * rows + feats) * parts, LANES), F32),
-            pltpu.VMEM((count * parts, LANES), F32),
-        ],
+        scratch_shapes=[pltpu.VMEM(((nout * rows + feats) * parts, LANES), F32)] * lots
+        + [pltpu.VMEM((count * parts, LANES), F32)],
         compiler_params=pltpu.CompilerParams(vmem_limit_bytes=60 * 1024 * 1024),
         name="scatter_add",
     )(idx, *pieces)
 
 
+def place_body(parts, at, *refs):
+    blocks, out = refs[:-1], refs[-1]
+    cols = blocks[0].shape[0]
+    me = at[0]
+    for core in range(2):
+        for m in range(parts):
+            ref = blocks[core * parts + m]
+            for j in range(cols):
+                out[(j * parts + m) * 2 + core ^ me] = ref[j]
+
+
+def place_blocks(me, blocks):
+    cols = blocks[0].shape[0]
+    shape = (len(blocks) * cols,) + blocks[0].shape[1:]
+    vm = pl.BlockSpec(memory_space=pltpu.VMEM)
+    return pl.pallas_call(
+        functools.partial(place_body, len(blocks) // 2),
+        out_shape=jax.ShapeDtypeStruct(shape, blocks[0].dtype),
+        in_specs=[pl.BlockSpec(memory_space=pltpu.SMEM)] + [vm] * len(blocks),
+        out_specs=vm,
+        name="place_blocks",
+    )(me.reshape(1), *blocks)
+
+
 SPLITS = 2
 GROUP_BYTES = 16 * 1024 * 1024
 
@@ -343,28 +375,54 @@
     return lax.ppermute(v, "dev", [(i, i ^ bits) for i in range(devices)])
 
 
-def sum_grad(grad, me, devices, block_rows):
-    bits = devices.bit_length() - 1
-    v = grad.reshape((2,) * bits + (block_rows, grad.shape[1]))
-    for b in range(bits):
-        axis = bits - 1 - b
-        mine = (me >> b) & 1
-        keep = lax.dynamic_index_in_dim(v, mine, axis, keepdims=False)
-        give = lax.dynamic_index_in_dim(v, 1 - mine, axis, keepdims=False)
-        v = keep + swap(give.astype(BF16), 1 << b).astype(F32)
-    return v
-
-
-def share_weights(v, me, devices):
-    bits = devices.bit_length() - 1
-    v = v[None]
-    for b in reversed(range(bits)):
-        got = swap(v, 1 << b)
-        high = ((me >> b) & 1) == 1
-        low_half = jnp.where(high, got, v)
-        high_half = jnp.where(high, v, got)
-        v = jnp.stack([low_half, high_half], axis=1).reshape((-1,) + v.shape[1:])
-    return v
+def gather_blocks(v, count, unit, direct):
+    got = [v] + [None] * (count - 1)
+    for k in range(1, count):
+        mate = k % 2 and k > 1 and not direct
+        got[k] = swap(got[k - 1], unit) if mate else swap(v, k * unit)
+    return got
+
+
+def merge_mates(outs, unit):
+    merged = []
+    for k in range(0, len(outs), 2):
+        merged.append(outs[k].astype(F32) + swap(outs[k + 1], unit).astype(F32))
+    return merged
+
+
+def reduce_blocks(outs, unit):
+    merged = merge_mates(outs, unit)
+    total = merged[0]
+    for i in range(1, len(merged)):
+        total = total + swap(merged[i].astype(BF16), 2 * i * unit).astype(F32)
+    return total
+
+
+def pick(v, at, axis):
+    return lax.dynamic_index_in_dim(v, at, axis, keepdims=False)
+
+
+def sum_grad(grad, me, group, columns, block_rows):
+    half = group // 2
+    v = grad.reshape(columns, half, 2, block_rows, grad.shape[1])
+    core, chip, column = me % 2, me // 2 % half, me // group
+    v = pick(v, core, 2) + swap(pick(v, 1 - core, 2).astype(BF16), 1).astype(F32)
+    total = pick(v, chip, 1)
+    for m in range(1, half):
+        total = total + swap(pick(v, chip ^ m, 1).astype(BF16), 2 * m).astype(F32)
+    v = total
+    total = pick(v, column, 0)
+    for k in range(1, columns):
+        total = total + swap(pick(v, column ^ k, 0).astype(BF16), k * group).astype(F32)
+    return total
+
+
+def share_weights(v, me, group, columns):
+    half = group // 2
+    v = jnp.stack([v] + [swap(v, k * group) for k in range(1, columns)])
+    near = [v] + [swap(v, 2 * m) for m in range(1, half)]
+    far = [swap(n, 1) for n in near]
+    return place_blocks(me, near + far)
 
 
 def shards(table, owners, local_rows, segments, cotangent, weights, master, moment1, moment2):
@@ -404,14 +462,14 @@
             sums, t = lax.optimization_barrier((sums, t))
         for m in range(0, group, 2):
             t[m + 1] = swap(t[m], 1)
+        index = [places(v, group * rows).reshape(-1) for v in all_ids]
         sums = [None] * columns
-        for k in reversed(range(columns)):
-            index = places(all_ids[k], group * rows).reshape(-1)
-            sums[k] = gather_sum(index, t, BF16 if k else F32, count)
-        total = sums[0]
-        for k in range(1, columns):
-            total = total + swap(sums[k], k * group).astype(F32)
-        x.append(total.astype(BF16))
+        for part in (range(3, columns, 2), (*range(2, columns, 2), 1, 0)):
+            kinds = [BF16 if k else F32 for k in part]
+            made = gather_sum(jnp.concatenate([index[k] for k in part]), t, kinds, count)
+            for k, s in zip(part, made):
+                sums[k] = s
+        x.append(reduce_blocks(sums, group).astype(BF16))
 
     out = dense(x, segments[0], weights, cotangent)
     dx, (normed, mixed, d_pre) = out[:SPLITS], out[SPLITS:]
@@ -420,27 +478,21 @@
     index = jnp.stack([places(v, spare) for v in all_ids]).reshape(-1)
     halves = []
     for n in range(SPLITS):
-        pieces = [dx[n]] + [swap(dx[n], k * group) for k in range(1, columns)]
+        pieces = gather_blocks(dx[n], columns, group, n > 0)
         outs = scatter_add(index, pieces, group, rows, (F32,) + (BF16,) * (group - 1))
-        merged = []
-        for m in range(0, group, 2):
-            merged.append(outs[m].astype(F32) + swap(outs[m + 1], 1).astype(F32))
-        total = merged[0]
-        for i, m in enumerate(range(2, group, 2)):
-            total = total + swap(merged[i + 1].astype(BF16), m).astype(F32)
-        halves.append(total)
+        halves.append(reduce_blocks(outs, 1))
     table_grad = jnp.concatenate(halves, axis=1)
 
     grad_in = jnp.dot(normed.T, d_pre, preferred_element_type=F32)
     grad_out = jnp.dot(mixed.T, cotangent, preferred_element_type=F32)
     full_grad = jnp.concatenate([grad_in, grad_out], axis=1)
-    grad = sum_grad(full_grad, me, devices, master.shape[0])
+    grad = sum_grad(full_grad, me, group, columns, master.shape[0])
     new_m1 = 0.9 * moment1 + 0.1 * grad
     new_m2 = 0.95 * moment2 + 0.05 * grad * grad
     fix1 = 1.0 - 0.9**10
     fix2 = 1.0 - 0.95**10
     new_master = master - 0.01 * (new_m1 / fix1) / (jnp.sqrt(new_m2 / fix2) + 1e-08)
-    new_weights = share_weights(new_master.astype(BF16), me, devices).reshape(weights.shape)
+    new_weights = share_weights(new_master.astype(BF16), me, group, columns).reshape(weights.shape)
     return (table_grad, new_weights, new_master, new_m1, new_m2)
 
 

time: 492 us -> 407 us (0.83)
  the two profiles are of different devices: /device:TPU:8 before, /device:TPU:0 now
where the time goes in v2:
time: 407 us
  waiting for transfers between devices  150 us (37%)
  Pallas kernels  148 us (36%)
  starting transfers between devices  71.1 us (17%)
  other arithmetic  20.3 us (5%)
  local copies, waits for them, and re-layouts  10.4 us (3%)
  matrix products  5.61 us (1%)
    ppermute x60, waiting for transfers between devices, swap(): return lax.ppermute(v, 'dev', [(i, i ^ bits) for i in range(devices)])  150 us
    ppermute x60, starting transfers between devices, swap(): return lax.ppermute(v, 'dev', [(i, i ^ bits) for i in range(devices)])  71.1 us
    pallas_call x2, Pallas kernels, scatter_add(): pl.pallas_call(functools.partial(scatter_body, len(pieces), nout, lots),...  51.6 us
    pallas_call x4, Pallas kernels, gather_sum(): pl.pallas_call(functools.partial(gather_body, len(tabs), len(dtypes), 8),...  50.1 us
    pallas_call x1, Pallas kernels, dense(): pl.pallas_call(functools.partial(dense_body, block, splits), out_shape=(j...  43.4 us
  transfers between devices with their start and end apart: 60, of which 26 were waited for; matrix products, arithmetic and copies ran while one was open for 7% of the time, Pallas kernels for 25%

profile of v2, /device:TPU:0, one launch (start us, length us, event | category | flops | bytes accessed | tf_op | source)
XLA Modules:
  0.0 406.6 jit_solution(17727609159788418302)
XLA Ops:
  1.9 3.0 collective-permute-start.4
  5.8 2.7 collective-permute-start.1
  12.0 5.7 %collective-permute-done.4.refs_2_ = bf16[1024,256]{1,0:T(8,128)(2,1)S(1)} collective-permute-done((bf16[1024,256]{1,0:T(8,128)(2,1)S(1)}, bf16[1024,256]{1,0:T(8,128)(2,1)S(1)}, u32[]{:S(2)}, u32[]{:S(2)}) %collective-permute-start.4) | collective-permute-done | bytes 524320 | tf_op jit(solution)/shard_map/ppermute | solution.py:375
  17.8 4.2 %collective-permute-start.2 = (s32[4,1024]{1,0:T(4,128)S(1)}, s32[4,1024]{1,0:T(4,128)S(1)}, u32[]{:S(2)}, u32[]{:S(2)}) collective-permute-start(s32[4,1024]{1,0:T(4,128)S(1)} %get-tuple-element.74), channel_id=1, source_target_pairs={{0,24},{1,25},{2,26},{3,27},{4,28},{5,29},{6,30},{7,31},{8,16},{9,... | collective-permute-start | bytes 49160 | tf_op jit(solution)/shard_map/ppermute | solution.py:375
  22.1 1.6 collective-permute-done.2
  23.7 1.7 collective-permute-start.13
  25.5 8.6 %collective-permute-done.6.refs_4_ = bf16[1024,256]{1,0:T(8,128)(2,1)S(1)} collective-permute-done((bf16[1024,256]{1,0:T(8,128)(2,1)S(1)}, bf16[1024,256]{1,0:T(8,128)(2,1)S(1)}, u32[]{:S(2)}, u32[]{:S(2)}) %collective-permute-start.6) | collective-permute-done | bytes 524320 | tf_op jit(solution)/shard_map/ppermute | solution.py:375
  38.9 17.0 %gather_sum.4 = (bf16[1024,256]{1,0:T(8,128)(2,1)}, bf16[1024,256]{1,0:T(8,128)(2,1)}, f32[1024,256]{1,0:T(8,128)}) custom-call(s32[12288]{0:T(1024)} %copy-done.38, bf16[1024,256]{1,0:T(8,128)(2,1)} %copy-done.3, bf16[1024,256]{1,0:T(8,128)(2,1)} %copy-done.10, bf16[1024,256]{1,0:T(8,128)(2,1)} %copy-done.4, bf16[1024,256]{1,0:T(8,128)(2,1)} %copy-done.11, ...), custom_call_target="tpu_custom_call" | custom-call | tf_op jit(solution)/shard_map/gather_sum/pallas_call | solution.py:275
  55.9 8.0 %gather_sum.5 = bf16[1024,256]{1,0:T(8,128)(2,1)} custom-call(s32[4096]{0:T(1024)} %bitcast.83, bf16[1024,256]{1,0:T(8,128)(2,1)} %copy-done.3, bf16[1024,256]{1,0:T(8,128)(2,1)} %copy-done.10, bf16[1024,256]{1,0:T(8,128)(2,1)} %copy-done.4, bf16[1024,256]{1,0:T(8,128)(2,1)} %copy-done.11, bf16[1024,256]{1,0:T(8,128)(2,1)} %copy-done.8, ...), custom_call_target="tpu_custom_call" | custom-call | tf_op jit(solution)/shard_map/gather_sum/pallas_call | solution.py:275
  68.4 8.1 %gather_sum.7 = bf16[1024,256]{1,0:T(8,128)(2,1)} custom-call(s32[4096]{0:T(1024)} %bitcast.84, bf16[1024,256]{1,0:T(8,128)(2,1)} %copy-done.2, bf16[1024,256]{1,0:T(8,128)(2,1)} %copy-done.12, bf16[1024,256]{1,0:T(8,128)(2,1)} %copy-done.5, bf16[1024,256]{1,0:T(8,128)(2,1)} %copy-done.13, bf16[1024,256]{1,0:T(8,128)(2,1)} %copy-done.6, ...), custom_call_target="tpu_custom_call" | custom-call | tf_op jit(solution)/shard_map/gather_sum/pallas_call | solution.py:275
  79.4 2.1 add_convert_fusion.9
  81.9 17.0 %gather_sum.6 = (bf16[1024,256]{1,0:T(8,128)(2,1)}, bf16[1024,256]{1,0:T(8,128)(2,1)}, f32[1024,256]{1,0:T(8,128)}) custom-call(s32[12288]{0:T(1024)} %copy-done.38, bf16[1024,256]{1,0:T(8,128)(2,1)} %copy-done.2, bf16[1024,256]{1,0:T(8,128)(2,1)} %copy-done.12, bf16[1024,256]{1,0:T(8,128)(2,1)} %copy-done.5, bf16[1024,256]{1,0:T(8,128)(2,1)} %copy-done.13, ...), custom_call_target="tpu_custom_call" | custom-call | tf_op jit(solution)/shard_map/gather_sum/pallas_call | solution.py:275
  100.3 2.5 collective-permute-done.21
  102.7 2.0 add_convert_fusion.7
  105.8 19.5 %collective-permute-done.10 = bf16[1024,256]{1,0:T(8,128)(2,1)S(1)} collective-permute-done((bf16[1024,256]{1,0:T(8,128)(2,1)}, bf16[1024,256]{1,0:T(8,128)(2,1)S(1)}, u32[]{:S(2)}, u32[]{:S(2)}) %collective-permute-start.10) | collective-permute-done | bytes 524320 | tf_op jit(solution)/shard_map/ppermute | solution.py:375
  126.2 9.5 %collective-permute-done.20 = bf16[1024,256]{1,0:T(8,128)(2,1)} collective-permute-done((bf16[1024,256]{1,0:T(8,128)(2,1)}, bf16[1024,256]{1,0:T(8,128)(2,1)}, u32[]{:S(2)}, u32[]{:S(2)}) %collective-permute-start.20) | collective-permute-done | bytes 524320 | tf_op jit(solution)/shard_map/ppermute | solution.py:375
  135.7 2.2 add_convert_fusion.6.refs_1_
  137.9 43.4 %dense_step.1 = (bf16[1024,256]{1,0:T(8,128)(2,1)}, bf16[1024,256]{1,0:T(8,128)(2,1)}, bf16[1024,512]{1,0:T(8,128)(2,1)}, bf16[1024,512]{1,0:T(8,128)(2,1)}, bf16[1024,2048]{1,0:T(8,128)(2,1)}) custom-call(bf16[1024,256]{1,0:T(8,128)(2,1)} %add_convert_fusion.8.refs_0_, bf16[1024,256]{1,0:T(8,128)(2,1)} %add_convert_fusion.6.refs_1_, ...), custom_call_target="tpu_custom_call" | custom-call | tf_op jit(solution)/shard_map/dense_step/pallas_call | solution.py:189
  183.0 2.7 collective-permute-start.35
  185.7 1.9 fusion.48
  187.6 3.7 fusion.47
  191.8 2.4 copy-done
  195.6 9.2 %collective-permute-done.33.refs_1_ = bf16[1024,256]{1,0:T(8,128)(2,1)S(1)} collective-permute-done((bf16[1024,256]{1,0:T(8,128)(2,1)}, bf16[1024,256]{1,0:T(8,128)(2,1)S(1)}, u32[]{:S(2)}, u32[]{:S(2)}) %collective-permute-start.33) | collective-permute-done | bytes 524320 | tf_op jit(solution)/shard_map/ppermute | solution.py:375
  204.8 26.6 %collective-permute-done.34.refs_2_ = bf16[1024,256]{1,0:T(8,128)(2,1)} collective-permute-done((bf16[1024,256]{1,0:T(8,128)(2,1)}, bf16[1024,256]{1,0:T(8,128)(2,1)}, u32[]{:S(2)}, u32[]{:S(2)}) %collective-permute-start.34) | collective-permute-done | bytes 524320 | tf_op jit(solution)/shard_map/ppermute | solution.py:375
  231.4 25.8 %scatter_add.3 = (f32[1024,256]{1,0:T(8,128)}, bf16[1024,256]{1,0:T(8,128)(2,1)}, bf16[1024,256]{1,0:T(8,128)(2,1)}, bf16[1024,256]{1,0:T(8,128)(2,1)}, bf16[102...) custom-call(s32[16384]{0:T(1024)} %bitcast.80, ...), custom_call_target="tpu_custom_call" | custom-call | tf_op jit(solution)/shard_map/scatter_add/pallas_call | solution.py:333
  257.2 11.8 %collective-permute-start.23 = (bf16[1024,256]{1,0:T(8,128)(2,1)}, bf16[1024,256]{1,0:T(8,128)(2,1)S(1)}, u32[]{:S(2)}, u32[]{:S(2)}) collective-permute-start(bf16[1024,256]{1,0:T(8,128)(2,1)} %get-tuple-element.46.refs_0_), channel_id=1, source_target_pairs={{0,8},{1,9},{2,10},{3,11},{4,12},{5,13},{6,14},{7,15},{8,0},{9,1},... | collective-permute-start | bytes 1572872 | tf_op jit(solution)/shard_map/ppermute | solution.py:375
  271.1 2.0 add_convert_fusion.2
  273.1 2.1 bitcast_add_fusion
  277.7 4.3 %collective-permute-done.23.refs_1_ = bf16[1024,256]{1,0:T(8,128)(2,1)S(1)} collective-permute-done((bf16[1024,256]{1,0:T(8,128)(2,1)}, bf16[1024,256]{1,0:T(8,128)(2,1)S(1)}, u32[]{:S(2)}, u32[]{:S(2)}) %collective-permute-start.23) | collective-permute-done | bytes 524320 | tf_op jit(solution)/shard_map/ppermute | solution.py:375
  285.1 8.0 %collective-permute-done.25.refs_3_ = bf16[1024,256]{1,0:T(8,128)(2,1)S(1)} collective-permute-done((bf16[1024,256]{1,0:T(8,128)(2,1)}, bf16[1024,256]{1,0:T(8,128)(2,1)S(1)}, u32[]{:S(2)}, u32[]{:S(2)}) %collective-permute-start.25) | collective-permute-done | bytes 524320 | tf_op jit(solution)/shard_map/ppermute | solution.py:375
  293.8 25.8 %scatter_add.2 = (f32[1024,256]{1,0:T(8,128)}, bf16[1024,256]{1,0:T(8,128)(2,1)}, bf16[1024,256]{1,0:T(8,128)(2,1)}, bf16[1024,256]{1,0:T(8,128)(2,1)}, bf16[102...) custom-call(s32[16384]{0:T(1024)} %bitcast.81, ...), custom_call_target="tpu_custom_call" | custom-call | tf_op jit(solution)/shard_map/scatter_add/pallas_call | solution.py:333
  323.0 1.8 collective-permute-start.47
  327.8 6.5 %collective-permute-done.48 = bf16[16,2560]{1,0:T(8,128)(2,1)S(1)} collective-permute-done((bf16[16,2560]{1,0:T(8,128)(2,1)S(1)}, bf16[16,2560]{1,0:T(8,128)(2,1)S(1)}, u32[]{:S(2)}, u32[]{:S(2)}) %collective-permute-start.48) | collective-permute-done | bytes 81952 | tf_op jit(solution)/shard_map/ppermute | solution.py:375
  336.7 1.6 collective-permute-start.50
  338.5 1.6 collective-permute-start.40
  342.1 7.2 %collective-permute-done.38 = bf16[1024,256]{1,0:T(8,128)(2,1)S(1)} collective-permute-done((bf16[1024,256]{1,0:T(8,128)(2,1)S(1)}, bf16[1024,256]{1,0:T(8,128)(2,1)S(1)}, u32[]{:S(2)}, u32[]{:S(2)}) %collective-permute-start.38) | collective-permute-done | bytes 524320 | tf_op jit(solution)/shard_map/ppermute | solution.py:375
  349.2 2.5 collective-permute-start.51
  353.3 3.2 collective-permute-done.51
  358.1 2.4 collective-permute-start.32
  360.6 3.5 collective-permute-done.40
  364.1 2.4 collective-permute-start.54
  366.5 5.3 %collective-permute-done.28 = bf16[1024,256]{1,0:T(8,128)(2,1)S(1)} collective-permute-done((bf16[1024,256]{1,0:T(8,128)(2,1)S(1)}, bf16[1024,256]{1,0:T(8,128)(2,1)S(1)}, u32[]{:S(2)}, u32[]{:S(2)}) %collective-permute-start.28) | collective-permute-done | bytes 524320 | tf_op jit(solution)/shard_map/ppermute | solution.py:375
  371.8 2.4 collective-permute-start.55
  375.5 11.0 %collective-permute-done.30 = bf16[1024,256]{1,0:T(8,128)(2,1)S(1)} collective-permute-done((bf16[1024,256]{1,0:T(8,128)(2,1)S(1)}, bf16[1024,256]{1,0:T(8,128)(2,1)S(1)}, u32[]{:S(2)}, u32[]{:S(2)}) %collective-permute-start.30) | collective-permute-done | bytes 524320 | tf_op jit(solution)/shard_map/ppermute | solution.py:375
  386.6 3.5 collective-permute-done.53.refs_1_
  390.1 9.0 %collective-permute-done.54.refs_2_ = bf16[4,16,2560]{2,1,0:T(8,128)(2,1)S(1)} collective-permute-done((bf16[4,16,2560]{2,1,0:T(8,128)(2,1)S(1)}, bf16[4,16,2560]{2,1,0:T(8,128)(2,1)S(1)}, u32[]{:S(2)}, u32[]{:S(2)}) %collective-permute-start.54) | collective-permute-done | bytes 327712 | tf_op jit(solution)/shard_map/ppermute | solution.py:375
  400.0 1.6 pad_maximum_fusion.1
  403.2 3.3 place_blocks.1
  (207 shorter events, 51.3 us)
Async XLA Ops:
  1.9 15.8 %collective-permute-start.4 = (bf16[1024,256]{1,0:T(8,128)(2,1)S(1)}, bf16[1024,256]{1,0:T(8,128)(2,1)S(1)}, u32[]{:S(2)}, u32[]{:S(2)}) collective-permute-start(bf16[1024,256]{1,0:T(8,128)(2,1)S(1)} %get-tuple-element.88.refs_0_), channel_id=1, source_target_pairs={{0,2},{1,3},{2,0},{3,1},{4,6},{5,7},{6,4},{7,5},{8,10},{9,11},{10,... | collective-permute-start | bytes 1572872 | tf_op jit(solution)/shard_map/ppermute | solution.py:375
  8.4 9.4 %collective-permute-start = (s32[4,1024]{1,0:T(4,128)S(1)}, s32[4,1024]{1,0:T(4,128)S(1)}, u32[]{:S(2)}, u32[]{:S(2)}) collective-permute-start(s32[4,1024]{1,0:T(4,128)S(1)} %get-tuple-element.74), channel_id=1, source_target_pairs={{0,8},{1,9},{2,10},{3,11},{4,12},{5,13},{6,14},{7,15},{8,0},{9,1},... | collective-permute-start | bytes 49160 | tf_op jit(solution)/shard_map/ppermute | solution.py:375
  10.0 24.1 %collective-permute-start.6 = (bf16[1024,256]{1,0:T(8,128)(2,1)S(1)}, bf16[1024,256]{1,0:T(8,128)(2,1)S(1)}, u32[]{:S(2)}, u32[]{:S(2)}) collective-permute-start(bf16[1024,256]{1,0:T(8,128)(2,1)S(1)} %get-tuple-element.88.refs_0_), channel_id=1, source_target_pairs={{0,4},{1,5},{2,6},{3,7},{4,0},{5,1},{6,2},{7,3},{8,12},{9,13},{10,... | collective-permute-start | bytes 1572872 | tf_op jit(solution)/shard_map/ppermute | solution.py:375
  11.5 24.1 %collective-permute-start.8 = (bf16[1024,256]{1,0:T(8,128)(2,1)S(1)}, bf16[1024,256]{1,0:T(8,128)(2,1)S(1)}, u32[]{:S(2)}, u32[]{:S(2)}) collective-permute-start(bf16[1024,256]{1,0:T(8,128)(2,1)S(1)} %get-tuple-element.88.refs_0_), channel_id=1, source_target_pairs={{0,6},{1,7},{2,4},{3,5},{4,2},{5,3},{6,0},{7,1},{8,14},{9,15},{10,... | collective-permute-start | bytes 1572872 | tf_op jit(solution)/shard_map/ppermute | solution.py:375
  12.0 24.1 %collective-permute-start.3 = (bf16[1024,256]{1,0:T(8,128)(2,1)S(1)}, bf16[1024,256]{1,0:T(8,128)(2,1)S(1)}, u32[]{:S(2)}, u32[]{:S(2)}) collective-permute-start(bf16[1024,256]{1,0:T(8,128)(2,1)S(1)} %get-tuple-element.88.refs_0_), channel_id=1, source_target_pairs={{0,1},{1,0},{2,3},{3,2},{4,5},{5,4},{6,7},{7,6},{8,9},{9,8},{10,11... | collective-permute-start | bytes 1572872 | tf_op jit(solution)/shard_map/ppermute | solution.py:375
  17.7 18.4 %collective-permute-start.5 = (bf16[1024,256]{1,0:T(8,128)(2,1)S(1)}, bf16[1024,256]{1,0:T(8,128)(2,1)S(1)}, u32[]{:S(2)}, u32[]{:S(2)}) collective-permute-start(bf16[1024,256]{1,0:T(8,128)(2,1)S(1)} %collective-permute-done.4.refs_2_), channel_id=1, source_target_pairs={{0,1},{1,0},{2,3},{3,2},{4,5},{5,4},{6,7},{7,6},{8,9},{9,8},{10,11... | collective-permute-start | bytes 1572872 | tf_op jit(solution)/shard_map/ppermute | solution.py:375
  23.7 40.2 %collective-permute-start.13 = (bf16[1024,256]{1,0:T(8,128)(2,1)S(1)}, bf16[1024,256]{1,0:T(8,128)(2,1)S(1)}, u32[]{:S(2)}, u32[]{:S(2)}) collective-permute-start(bf16[1024,256]{1,0:T(8,128)(2,1)S(1)} %get-tuple-element.39.refs_0_), channel_id=1, source_target_pairs={{0,2},{1,3},{2,0},{3,1},{4,6},{5,7},{6,4},{7,5},{8,10},{9,11},{10,... | collective-permute-start | bytes 1572872 | tf_op jit(solution)/shard_map/ppermute | solution.py:375
  34.1 29.9 %collective-permute-start.14 = (bf16[1024,256]{1,0:T(8,128)(2,1)S(1)}, bf16[1024,256]{1,0:T(8,128)(2,1)S(1)}, u32[]{:S(2)}, u32[]{:S(2)}) collective-permute-start(bf16[1024,256]{1,0:T(8,128)(2,1)S(1)} %get-tuple-element.39.refs_0_), channel_id=1, source_target_pairs={{0,4},{1,5},{2,6},{3,7},{4,0},{5,1},{6,2},{7,3},{8,12},{9,13},{10,... | collective-permute-start | bytes 1572872 | tf_op jit(solution)/shard_map/ppermute | solution.py:375
  35.6 28.4 %collective-permute-start.15 = (bf16[1024,256]{1,0:T(8,128)(2,1)S(1)}, bf16[1024,256]{1,0:T(8,128)(2,1)S(1)}, u32[]{:S(2)}, u32[]{:S(2)}) collective-permute-start(bf16[1024,256]{1,0:T(8,128)(2,1)S(1)} %get-tuple-element.39.refs_0_), channel_id=1, source_target_pairs={{0,6},{1,7},{2,4},{3,5},{4,2},{5,3},{6,0},{7,1},{8,14},{9,15},{10,... | collective-permute-start | bytes 1572872 | tf_op jit(solution)/shard_map/ppermute | solution.py:375
  65.1 14.3 %collective-permute-start.11 = (bf16[1024,256]{1,0:T(8,128)(2,1)}, bf16[1024,256]{1,0:T(8,128)(2,1)}, u32[]{:S(2)}, u32[]{:S(2)}) collective-permute-start(bf16[1024,256]{1,0:T(8,128)(2,1)} %gather_sum.5), channel_id=1, source_target_pairs={{0,8},{1,9},{2,10},{3,11},{4,12},{5,13},{6,14},{7,15},{8,0},{9,1},... | collective-permute-start | bytes 1572872 | tf_op jit(solution)/shard_map/ppermute | solution.py:375
  76.5 26.2 %collective-permute-start.21 = (bf16[1024,256]{1,0:T(8,128)(2,1)}, bf16[1024,256]{1,0:T(8,128)(2,1)S(1)}, u32[]{:S(2)}, u32[]{:S(2)}) collective-permute-start(bf16[1024,256]{1,0:T(8,128)(2,1)} %gather_sum.7), channel_id=1, source_target_pairs={{0,8},{1,9},{2,10},{3,11},{4,12},{5,13},{6,14},{7,15},{8,0},{9,1},... | collective-permute-start | bytes 1572872 | tf_op jit(solution)/shard_map/ppermute | solution.py:375
  76.9 48.3 %collective-permute-start.10 = (bf16[1024,256]{1,0:T(8,128)(2,1)}, bf16[1024,256]{1,0:T(8,128)(2,1)S(1)}, u32[]{:S(2)}, u32[]{:S(2)}) collective-permute-start(bf16[1024,256]{1,0:T(8,128)(2,1)} %get-tuple-element.37), channel_id=1, source_target_pairs={{0,8},{1,9},{2,10},{3,11},{4,12},{5,13},{6,14},{7,15},{8,0},{9,1},... | collective-permute-start | bytes 1572872 | tf_op jit(solution)/shard_map/ppermute | solution.py:375
  81.5 43.7 %collective-permute-start.12 = (bf16[1024,256]{1,0:T(8,128)(2,1)}, bf16[1024,256]{1,0:T(8,128)(2,1)S(1)}, u32[]{:S(2)}, u32[]{:S(2)}) collective-permute-start(bf16[1024,256]{1,0:T(8,128)(2,1)} %add_convert_fusion.9), channel_id=1, source_target_pairs={{0,16},{1,17},{2,18},{3,19},{4,20},{5,21},{6,22},{7,23},{8,24},{9,... | collective-permute-start | bytes 1572872 | tf_op jit(solution)/shard_map/ppermute | solution.py:375
  98.9 36.8 %collective-permute-start.20 = (bf16[1024,256]{1,0:T(8,128)(2,1)}, bf16[1024,256]{1,0:T(8,128)(2,1)}, u32[]{:S(2)}, u32[]{:S(2)}) collective-permute-start(bf16[1024,256]{1,0:T(8,128)(2,1)} %get-tuple-element.44), channel_id=1, source_target_pairs={{0,8},{1,9},{2,10},{3,11},{4,12},{5,13},{6,14},{7,15},{8,0},{9,1},... | collective-permute-start | bytes 1572872 | tf_op jit(solution)/shard_map/ppermute | solution.py:375
  104.7 31.0 %collective-permute-start.22 = (bf16[1024,256]{1,0:T(8,128)(2,1)}, bf16[1024,256]{1,0:T(8,128)(2,1)}, u32[]{:S(2)}, u32[]{:S(2)}) collective-permute-start(bf16[1024,256]{1,0:T(8,128)(2,1)} %add_convert_fusion.7), channel_id=1, source_target_pairs={{0,16},{1,17},{2,18},{3,19},{4,20},{5,21},{6,22},{7,23},{8,24},{9,... | collective-permute-start | bytes 1572872 | tf_op jit(solution)/shard_map/ppermute | solution.py:375
  181.3 23.5 %collective-permute-start.33 = (bf16[1024,256]{1,0:T(8,128)(2,1)}, bf16[1024,256]{1,0:T(8,128)(2,1)S(1)}, u32[]{:S(2)}, u32[]{:S(2)}) collective-permute-start(bf16[1024,256]{1,0:T(8,128)(2,1)} %get-tuple-element.55.refs_0_), channel_id=1, source_target_pairs={{0,8},{1,9},{2,10},{3,11},{4,12},{5,13},{6,14},{7,15},{8,0},{9,1},... | collective-permute-start | bytes 1572872 | tf_op jit(solution)/shard_map/ppermute | solution.py:375
  181.7 49.7 %collective-permute-start.34 = (bf16[1024,256]{1,0:T(8,128)(2,1)}, bf16[1024,256]{1,0:T(8,128)(2,1)}, u32[]{:S(2)}, u32[]{:S(2)}) collective-permute-start(bf16[1024,256]{1,0:T(8,128)(2,1)} %get-tuple-element.55.refs_0_), channel_id=1, source_target_pairs={{0,16},{1,17},{2,18},{3,19},{4,20},{5,21},{6,22},{7,23},{8,24},{9,... | collective-permute-start | bytes 1572872 | tf_op jit(solution)/shard_map/ppermute | solution.py:375
  183.0 48.4 %collective-permute-start.35 = (bf16[1024,256]{1,0:T(8,128)(2,1)}, bf16[1024,256]{1,0:T(8,128)(2,1)}, u32[]{:S(2)}, u32[]{:S(2)}) collective-permute-start(bf16[1024,256]{1,0:T(8,128)(2,1)} %get-tuple-element.55.refs_0_), channel_id=1, source_target_pairs={{0,24},{1,25},{2,26},{3,27},{4,28},{5,29},{6,30},{7,31},{8,16},{9,... | collective-permute-start | bytes 1572872 | tf_op jit(solution)/shard_map/ppermute | solution.py:375
  194.3 78.8 %collective-permute-start.43 = (bf16[4,4,16,2560]{3,2,0,1:T(8,128)(2,1)S(1)}, bf16[4,4,16,2560]{3,2,0,1:T(8,128)(2,1)S(1)}, u32[]{:S(2)}, u32[]{:S(2)}) collective-permute-start(bf16[4,4,16,2560]{3,2,0,1:T(8,128)(2,1)S(1)} %fusion), channel_id=1, source_target_pairs={{0,1},{1,0},{2,3},{3,2},{4,5},{5,4},{6,7},{7,6},{8,9},{9,8},{10,11... | collective-permute-start | bytes 3932168 | tf_op jit(solution)/shard_map/ppermute | solution.py:375
  195.1 74.1 %collective-permute-start.24 = (bf16[1024,256]{1,0:T(8,128)(2,1)}, bf16[1024,256]{1,0:T(8,128)(2,1)}, u32[]{:S(2)}, u32[]{:S(2)}) collective-permute-start(bf16[1024,256]{1,0:T(8,128)(2,1)} %get-tuple-element.46.refs_0_), channel_id=1, source_target_pairs={{0,16},{1,17},{2,18},{3,19},{4,20},{5,21},{6,22},{7,23},{8,24},{9,... | collective-permute-start | bytes 1572872 | tf_op jit(solution)/shard_map/ppermute | solution.py:375
  257.2 12.4 %collective-permute-start.37 = (bf16[1024,256]{1,0:T(8,128)(2,1)}, bf16[1024,256]{1,0:T(8,128)(2,1)S(1)}, u32[]{:S(2)}, u32[]{:S(2)}) collective-permute-start(bf16[1024,256]{1,0:T(8,128)(2,1)} %get-tuple-element.59), channel_id=1, source_target_pairs={{0,1},{1,0},{2,3},{3,2},{4,5},{5,4},{6,7},{7,6},{8,9},{9,8},{10,11... | collective-permute-start | bytes 1572872 | tf_op jit(solution)/shard_map/ppermute | solution.py:375
  257.2 24.8 %collective-permute-start.23 = (bf16[1024,256]{1,0:T(8,128)(2,1)}, bf16[1024,256]{1,0:T(8,128)(2,1)S(1)}, u32[]{:S(2)}, u32[]{:S(2)}) collective-permute-start(bf16[1024,256]{1,0:T(8,128)(2,1)} %get-tuple-element.46.refs_0_), channel_id=1, source_target_pairs={{0,8},{1,9},{2,10},{3,11},{4,12},{5,13},{6,14},{7,15},{8,0},{9,1},... | collective-permute-start | bytes 1572872 | tf_op jit(solution)/shard_map/ppermute | solution.py:375
  269.0 14.6 %collective-permute-start.39 = (bf16[1024,256]{1,0:T(8,128)(2,1)}, bf16[1024,256]{1,0:T(8,128)(2,1)S(1)}, u32[]{:S(2)}, u32[]{:S(2)}) collective-permute-start(bf16[1024,256]{1,0:T(8,128)(2,1)} %get-tuple-element.61), channel_id=1, source_target_pairs={{0,1},{1,0},{2,3},{3,2},{4,5},{5,4},{6,7},{7,6},{8,9},{9,8},{10,11... | collective-permute-start | bytes 1572872 | tf_op jit(solution)/shard_map/ppermute | solution.py:375
  269.2 50.4 %collective-permute-start.41 = (bf16[1024,256]{1,0:T(8,128)(2,1)}, bf16[1024,256]{1,0:T(8,128)(2,1)}, u32[]{:S(2)}, u32[]{:S(2)}) collective-permute-start(bf16[1024,256]{1,0:T(8,128)(2,1)} %get-tuple-element.63), channel_id=1, source_target_pairs={{0,1},{1,0},{2,3},{3,2},{4,5},{5,4},{6,7},{7,6},{8,9},{9,8},{10,11... | collective-permute-start | bytes 1572872 | tf_op jit(solution)/shard_map/ppermute | solution.py:375
  269.6 23.5 %collective-permute-start.25 = (bf16[1024,256]{1,0:T(8,128)(2,1)}, bf16[1024,256]{1,0:T(8,128)(2,1)S(1)}, u32[]{:S(2)}, u32[]{:S(2)}) collective-permute-start(bf16[1024,256]{1,0:T(8,128)(2,1)} %collective-permute-done.24.refs_2_), channel_id=1, source_target_pairs={{0,8},{1,9},{2,10},{3,11},{4,12},{5,13},{6,14},{7,15},{8,0},{9,1},... | collective-permute-start | bytes 1572872 | tf_op jit(solution)/shard_map/ppermute | solution.py:375
  276.3 45.2 %collective-permute-start.44 = (bf16[4,16,2560]{2,1,0:T(8,128)(2,1)}, bf16[4,16,2560]{2,1,0:T(8,128)(2,1)S(1)}, u32[]{:S(2)}, u32[]{:S(2)}) collective-permute-start(bf16[4,16,2560]{2,1,0:T(8,128)(2,1)} %get-tuple-element.84), channel_id=1, source_target_pairs={{0,2},{1,3},{2,0},{3,1},{4,6},{5,7},{6,4},{7,5},{8,10},{9,11},{10,... | collective-permute-start | bytes 983048 | tf_op jit(solution)/shard_map/ppermute | solution.py:375
  282.0 39.7 %collective-permute-start.45 = (bf16[4,16,2560]{2,1,0:T(8,128)(2,1)}, bf16[4,16,2560]{2,1,0:T(8,128)(2,1)}, u32[]{:S(2)}, u32[]{:S(2)}) collective-permute-start(bf16[4,16,2560]{2,1,0:T(8,128)(2,1)} %get-tuple-element.86), channel_id=1, source_target_pairs={{0,4},{1,5},{2,6},{3,7},{4,0},{5,1},{6,2},{7,3},{8,12},{9,13},{10,... | collective-permute-start | bytes 983048 | tf_op jit(solution)/shard_map/ppermute | solution.py:375
  283.6 38.1 %collective-permute-start.46 = (bf16[4,16,2560]{2,1,0:T(8,128)(2,1)}, bf16[4,16,2560]{2,1,0:T(8,128)(2,1)}, u32[]{:S(2)}, u32[]{:S(2)}) collective-permute-start(bf16[4,16,2560]{2,1,0:T(8,128)(2,1)} %get-tuple-element.85), channel_id=1, source_target_pairs={{0,6},{1,7},{2,4},{3,5},{4,2},{5,3},{6,0},{7,1},{8,14},{9,15},{10,... | collective-permute-start | bytes 983048 | tf_op jit(solution)/shard_map/ppermute | solution.py:375
  293.8 44.7 %collective-permute-start.36 = (bf16[1024,256]{1,0:T(8,128)(2,1)}, bf16[1024,256]{1,0:T(8,128)(2,1)}, u32[]{:S(2)}, u32[]{:S(2)}) collective-permute-start(bf16[1024,256]{1,0:T(8,128)(2,1)} %get-tuple-element.57), channel_id=1, source_target_pairs={{0,1},{1,0},{2,3},{3,2},{4,5},{5,4},{6,7},{7,6},{8,9},{9,8},{10,11... | collective-permute-start | bytes 1572872 | tf_op jit(solution)/shard_map/ppermute | solution.py:375
  319.6 6.4 %collective-permute-start.27 = (bf16[1024,256]{1,0:T(8,128)(2,1)}, bf16[1024,256]{1,0:T(8,128)(2,1)S(1)}, u32[]{:S(2)}, u32[]{:S(2)}) collective-permute-start(bf16[1024,256]{1,0:T(8,128)(2,1)} %get-tuple-element.50), channel_id=1, source_target_pairs={{0,1},{1,0},{2,3},{3,2},{4,5},{5,4},{6,7},{7,6},{8,9},{9,8},{10,11... | collective-permute-start | bytes 1572872 | tf_op jit(solution)/shard_map/ppermute | solution.py:375
  321.6 15.1 %collective-permute-start.29 = (bf16[1024,256]{1,0:T(8,128)(2,1)}, bf16[1024,256]{1,0:T(8,128)(2,1)S(1)}, u32[]{:S(2)}, u32[]{:S(2)}) collective-permute-start(bf16[1024,256]{1,0:T(8,128)(2,1)} %get-tuple-element.52), channel_id=1, source_target_pairs={{0,1},{1,0},{2,3},{3,2},{4,5},{5,4},{6,7},{7,6},{8,9},{9,8},{10,11... | collective-permute-start | bytes 1572872 | tf_op jit(solution)/shard_map/ppermute | solution.py:375
  324.8 9.5 %collective-permute-start.48 = (bf16[16,2560]{1,0:T(8,128)(2,1)S(1)}, bf16[16,2560]{1,0:T(8,128)(2,1)S(1)}, u32[]{:S(2)}, u32[]{:S(2)}) collective-permute-start(bf16[16,2560]{1,0:T(8,128)(2,1)S(1)} %get-tuple-element.91), channel_id=1, source_target_pairs={{0,16},{1,17},{2,18},{3,19},{4,20},{5,21},{6,22},{7,23},{8,24},{9,... | collective-permute-start | bytes 245768 | tf_op jit(solution)/shard_map/ppermute | solution.py:375
  326.0 8.3 %collective-permute-start.49 = (bf16[16,2560]{1,0:T(8,128)(2,1)S(1)}, bf16[16,2560]{1,0:T(8,128)(2,1)S(1)}, u32[]{:S(2)}, u32[]{:S(2)}) collective-permute-start(bf16[16,2560]{1,0:T(8,128)(2,1)S(1)} %get-tuple-element.90), channel_id=1, source_target_pairs={{0,24},{1,25},{2,26},{3,27},{4,28},{5,29},{6,30},{7,31},{8,16},{9,... | collective-permute-start | bytes 245768 | tf_op jit(solution)/shard_map/ppermute | solution.py:375
  327.8 12.3 %collective-permute-start.31 = (bf16[1024,256]{1,0:T(8,128)(2,1)S(1)}, bf16[1024,256]{1,0:T(8,128)(2,1)S(1)}, u32[]{:S(2)}, u32[]{:S(2)}) collective-permute-start(bf16[1024,256]{1,0:T(8,128)(2,1)S(1)} %copy-done.44), channel_id=1, source_target_pairs={{0,1},{1,0},{2,3},{3,2},{4,5},{5,4},{6,7},{7,6},{8,9},{9,8},{10,11... | collective-permute-start | bytes 1572872 | tf_op jit(solution)/shard_map/ppermute | solution.py:375
  334.4 14.9 %collective-permute-start.38 = (bf16[1024,256]{1,0:T(8,128)(2,1)S(1)}, bf16[1024,256]{1,0:T(8,128)(2,1)S(1)}, u32[]{:S(2)}, u32[]{:S(2)}) collective-permute-start(bf16[1024,256]{1,0:T(8,128)(2,1)S(1)} %copy-done.23), channel_id=1, source_target_pairs={{0,2},{1,3},{2,0},{3,1},{4,6},{5,7},{6,4},{7,5},{8,10},{9,11},{10,... | collective-permute-start | bytes 1572872 | tf_op jit(solution)/shard_map/ppermute | solution.py:375
  336.7 15.1 %collective-permute-start.50 = (bf16[16,2560]{1,0:T(8,128)(2,1)S(1)}, bf16[16,2560]{1,0:T(8,128)(2,1)S(1)}, u32[]{:S(2)}, u32[]{:S(2)}) collective-permute-start(bf16[16,2560]{1,0:T(8,128)(2,1)S(1)} %get-tuple-element.67), channel_id=1, source_target_pairs={{0,8},{1,9},{2,10},{3,11},{4,12},{5,13},{6,14},{7,15},{8,0},{9,1},... | collective-permute-start | bytes 245768 | tf_op jit(solution)/shard_map/ppermute | solution.py:375
  338.5 25.6 %collective-permute-start.40 = (bf16[1024,256]{1,0:T(8,128)(2,1)S(1)}, bf16[1024,256]{1,0:T(8,128)(2,1)S(1)}, u32[]{:S(2)}, u32[]{:S(2)}) collective-permute-start(bf16[1024,256]{1,0:T(8,128)(2,1)S(1)} %add_convert_fusion.1), channel_id=1, source_target_pairs={{0,4},{1,5},{2,6},{3,7},{4,0},{5,1},{6,2},{7,3},{8,12},{9,13},{10,... | collective-permute-start | bytes 1572872 | tf_op jit(solution)/shard_map/ppermute | solution.py:375
  340.1 24.0 %collective-permute-start.42 = (bf16[1024,256]{1,0:T(8,128)(2,1)S(1)}, bf16[1024,256]{1,0:T(8,128)(2,1)S(1)}, u32[]{:S(2)}, u32[]{:S(2)}) collective-permute-start(bf16[1024,256]{1,0:T(8,128)(2,1)S(1)} %add_convert_fusion), channel_id=1, source_target_pairs={{0,6},{1,7},{2,4},{3,5},{4,2},{5,3},{6,0},{7,1},{8,14},{9,15},{10,... | collective-permute-start | bytes 1572872 | tf_op jit(solution)/shard_map/ppermute | solution.py:375
  340.6 31.1 %collective-permute-start.28 = (bf16[1024,256]{1,0:T(8,128)(2,1)S(1)}, bf16[1024,256]{1,0:T(8,128)(2,1)S(1)}, u32[]{:S(2)}, u32[]{:S(2)}) collective-permute-start(bf16[1024,256]{1,0:T(8,128)(2,1)S(1)} %add_convert_fusion.5), channel_id=1, source_target_pairs={{0,2},{1,3},{2,0},{3,1},{4,6},{5,7},{6,4},{7,5},{8,10},{9,11},{10,... | collective-permute-start | bytes 1572872 | tf_op jit(solution)/shard_map/ppermute | solution.py:375
  349.2 7.3 %collective-permute-start.51 = (bf16[16,2560]{1,0:T(8,128)(2,1)S(1)}, bf16[16,2560]{1,0:T(8,128)(2,1)S(1)}, u32[]{:S(2)}, u32[]{:S(2)}) collective-permute-start(bf16[16,2560]{1,0:T(8,128)(2,1)S(1)} %get-tuple-element.67), channel_id=1, source_target_pairs={{0,16},{1,17},{2,18},{3,19},{4,20},{5,21},{6,22},{7,23},{8,24},{9,... | collective-permute-start | bytes 245768 | tf_op jit(solution)/shard_map/ppermute | solution.py:375
  351.8 6.4 %collective-permute-start.52 = (bf16[16,2560]{1,0:T(8,128)(2,1)S(1)}, bf16[16,2560]{1,0:T(8,128)(2,1)S(1)}, u32[]{:S(2)}, u32[]{:S(2)}) collective-permute-start(bf16[16,2560]{1,0:T(8,128)(2,1)S(1)} %get-tuple-element.67), channel_id=1, source_target_pairs={{0,24},{1,25},{2,26},{3,27},{4,28},{5,29},{6,30},{7,31},{8,16},{9,... | collective-permute-start | bytes 245768 | tf_op jit(solution)/shard_map/ppermute | solution.py:375
  356.6 30.0 %collective-permute-start.30 = (bf16[1024,256]{1,0:T(8,128)(2,1)S(1)}, bf16[1024,256]{1,0:T(8,128)(2,1)S(1)}, u32[]{:S(2)}, u32[]{:S(2)}) collective-permute-start(bf16[1024,256]{1,0:T(8,128)(2,1)S(1)} %add_convert_fusion.4), channel_id=1, source_target_pairs={{0,4},{1,5},{2,6},{3,7},{4,0},{5,1},{6,2},{7,3},{8,12},{9,13},{10,... | collective-permute-start | bytes 1572872 | tf_op jit(solution)/shard_map/ppermute | solution.py:375
  358.1 41.5 %collective-permute-start.32 = (bf16[1024,256]{1,0:T(8,128)(2,1)S(1)}, bf16[1024,256]{1,0:T(8,128)(2,1)S(1)}, u32[]{:S(2)}, u32[]{:S(2)}) collective-permute-start(bf16[1024,256]{1,0:T(8,128)(2,1)S(1)} %add_convert_fusion.3), channel_id=1, source_target_pairs={{0,6},{1,7},{2,4},{3,5},{4,2},{5,3},{6,0},{7,1},{8,14},{9,15},{10,... | collective-permute-start | bytes 1572872 | tf_op jit(solution)/shard_map/ppermute | solution.py:375
  364.1 26.0 %collective-permute-start.53 = (bf16[4,16,2560]{2,1,0:T(8,128)(2,1)S(1)}, bf16[4,16,2560]{2,1,0:T(8,128)(2,1)S(1)}, u32[]{:S(2)}, u32[]{:S(2)}) collective-permute-start(bf16[4,16,2560]{2,1,0:T(8,128)(2,1)S(1)} %pad_maximum_fusion.2.refs_0_), channel_id=1, source_target_pairs={{0,2},{1,3},{2,0},{3,1},{4,6},{5,7},{6,4},{7,5},{8,10},{9,11},{10,... | collective-permute-start | bytes 983048 | tf_op jit(solution)/shard_map/ppermute | solution.py:375
  364.1 35.0 %collective-permute-start.54 = (bf16[4,16,2560]{2,1,0:T(8,128)(2,1)S(1)}, bf16[4,16,2560]{2,1,0:T(8,128)(2,1)S(1)}, u32[]{:S(2)}, u32[]{:S(2)}) collective-permute-start(bf16[4,16,2560]{2,1,0:T(8,128)(2,1)S(1)} %pad_maximum_fusion.2.refs_0_), channel_id=1, source_target_pairs={{0,4},{1,5},{2,6},{3,7},{4,0},{5,1},{6,2},{7,3},{8,12},{9,13},{10,... | collective-permute-start | bytes 983048 | tf_op jit(solution)/shard_map/ppermute | solution.py:375
  371.8 27.4 %collective-permute-start.55 = (bf16[4,16,2560]{2,1,0:T(8,128)(2,1)S(1)}, bf16[4,16,2560]{2,1,0:T(8,128)(2,1)S(1)}, u32[]{:S(2)}, u32[]{:S(2)}) collective-permute-start(bf16[4,16,2560]{2,1,0:T(8,128)(2,1)S(1)} %pad_maximum_fusion.2.refs_0_), channel_id=1, source_target_pairs={{0,6},{1,7},{2,4},{3,5},{4,2},{5,3},{6,0},{7,1},{8,14},{9,15},{10,... | collective-permute-start | bytes 983048 | tf_op jit(solution)/shard_map/ppermute | solution.py:375
  386.6 15.1 %collective-permute-start.56 = (bf16[4,16,2560]{2,1,0:T(8,128)(2,1)S(1)}, bf16[4,16,2560]{2,1,0:T(8,128)(2,1)S(1)}, u32[]{:S(2)}, u32[]{:S(2)}) collective-permute-start(bf16[4,16,2560]{2,1,0:T(8,128)(2,1)S(1)} %pad_maximum_fusion.2.refs_0_), channel_id=1, source_target_pairs={{0,1},{1,0},{2,3},{3,2},{4,5},{5,4},{6,7},{7,6},{8,9},{9,8},{10,11... | collective-permute-start | bytes 983048 | tf_op jit(solution)/shard_map/ppermute | solution.py:375
  390.1 11.6 %collective-permute-start.57 = (bf16[4,16,2560]{2,1,0:T(8,128)(2,1)S(1)}, bf16[4,16,2560]{2,1,0:T(8,128)(2,1)S(1)}, u32[]{:S(2)}, u32[]{:S(2)}) collective-permute-start(bf16[4,16,2560]{2,1,0:T(8,128)(2,1)S(1)} %collective-permute-done.53.refs_1_), channel_id=1, source_target_pairs={{0,1},{1,0},{2,3},{3,2},{4,5},{5,4},{6,7},{7,6},{8,9},{9,8},{10,11... | collective-permute-start | bytes 983048 | tf_op jit(solution)/shard_map/ppermute | solution.py:375
  (57 other events, 728.2 us)

commit v3 on v2

--- a/solution.py
+++ b/solution.py
@@ -287,8 +287,8 @@
 
 
 def scatter_body(npiece, nout, lots, idx, *refs):
-    pieces, outs = refs[:npiece], refs[npiece:npiece + nout]
-    accs, stage = refs[npiece + nout:-1], refs[-1]
+    pieces, outs, far = refs[:npiece], refs[npiece:npiece + nout // 2], refs[npiece + nout // 2]
+    accs, stage = refs[npiece + nout // 2 + 1:-1], refs[-1]
     count, width = pieces[0].shape
     rows = outs[0].shape[0]
     parts = width // LANES
@@ -320,8 +320,9 @@
             return c
 
         lax.fori_loop(0, count // (2 * lots), step, 0)
-    for o in range(nout):
-        join_rows(outs[o], accs, o * rows, chunk)
+    for o in range(nout // 2):
+        join_rows(outs[o], accs, 2 * o * rows, chunk)
+        join_rows(far.at[o], accs, (2 * o + 1) * rows, chunk)
 
 
 def scatter_add(idx, pieces, nout, rows, dtypes):
@@ -332,9 +333,10 @@
     vm = pl.BlockSpec(memory_space=pltpu.VMEM)
     return pl.pallas_call(
         functools.partial(scatter_body, len(pieces), nout, lots),
-        out_shape=tuple(jax.ShapeDtypeStruct((rows, width), d) for d in dtypes),
+        out_shape=tuple(jax.ShapeDtypeStruct((rows, width), d) for d in dtypes)
+        + (jax.ShapeDtypeStruct((nout // 2, rows, width), BF16),),
         in_specs=[pl.BlockSpec(memory_space=pltpu.SMEM)] + [vm] * len(pieces),
-        out_specs=(vm,) * nout,
+        out_specs=(vm,) * (nout // 2 + 1),
         scratch_shapes=[pltpu.VMEM(((nout * rows + feats) * parts, LANES), F32)] * lots
         + [pltpu.VMEM((count * parts, LANES), F32)],
         compiler_params=pltpu.CompilerParams(vmem_limit_bytes=60 * 1024 * 1024),
@@ -383,18 +385,12 @@
     return got
 
 
-def merge_mates(outs, unit):
-    merged = []
-    for k in range(0, len(outs), 2):
-        merged.append(outs[k].astype(F32) + swap(outs[k + 1], unit).astype(F32))
-    return merged
-
-
-def reduce_blocks(outs, unit):
-    merged = merge_mates(outs, unit)
+def reduce_blocks(near, far, unit):
+    merged = [v.astype(F32) + f.astype(F32) for v, f in zip(near, far)]
     total = merged[0]
     for i in range(1, len(merged)):
-        total = total + swap(merged[i].astype(BF16), 2 * i * unit).astype(F32)
+        give = merged[i].astype(BF16)
+        total = total + swap(give, 2 * i * unit).astype(F32)
     return total
 
 
@@ -469,7 +465,8 @@
             made = gather_sum(jnp.concatenate([index[k] for k in part]), t, kinds, count)
             for k, s in zip(part, made):
                 sums[k] = s
-        x.append(reduce_blocks(sums, group).astype(BF16))
+        far = [swap(s, group) for s in sums[1::2]]
+        x.append(reduce_blocks(sums[0::2], far, group).astype(BF16))
 
     out = dense(x, segments[0], weights, cotangent)
     dx, (normed, mixed, d_pre) = out[:SPLITS], out[SPLITS:]
@@ -479,8 +476,9 @@
     halves = []
     for n in range(SPLITS):
         pieces = gather_blocks(dx[n], columns, group, n > 0)
-        outs = scatter_add(index, pieces, group, rows, (F32,) + (BF16,) * (group - 1))
-        halves.append(reduce_blocks(outs, 1))
+        outs = scatter_add(index, pieces, group, rows, (F32,) + (BF16,) * (group // 2 - 1))
+        far = swap(outs[-1], 1)
+        halves.append(reduce_blocks(outs[:-1], [far[i] for i in range(group // 2)], 1))
     table_grad = jnp.concatenate(halves, axis=1)
 
     grad_in = jnp.dot(normed.T, d_pre, preferred_element_type=F32)

time: 407 us -> 409 us (level)
  starting transfers between devices: 71.1 us -> 62.9 us
  other arithmetic: 20.3 us -> 26.5 us
    ppermute x60 -> x54, starting transfers between devices: 71.1 us -> 62.9 us  [swap(): return lax.ppermute(v, 'dev', [(i, i ^ bits) for i in range(devices)])]
    ppermute x60 -> x54, waiting for transfers between devices: 150 us -> 153 us  [swap(): return lax.ppermute(v, 'dev', [(i, i ^ bits) for i in range(devices)])]
    convert_element_type x10 -> x6, other arithmetic: 11.1 us -> 12 us  [the longest x4 8.92 us: reduce_blocks(): give = merged[i].astype(BF16)]
  transfers between devices with their start and end apart: 60 -> 54, of which waited for: 26 -> 26; matrix products, arithmetic and copies ran while one was open for 7% -> 6% of each run, Pallas kernels for 25% -> 26%
where the time goes in v3:
time: 409 us; the launch traced here: 407 us
  waiting for transfers between devices  153 us (37%)
  Pallas kernels  149 us (36%)
  starting transfers between devices  62.9 us (15%)
  other arithmetic  26.5 us (6%)
  local copies, waits for them, and re-layouts  9.22 us (2%)
  matrix products  5.76 us (1%)
    ppermute x54, waiting for transfers between devices, swap(): return lax.ppermute(v, 'dev', [(i, i ^ bits) for i in range(devices)])  153 us
    ppermute x54, starting transfers between devices, swap(): return lax.ppermute(v, 'dev', [(i, i ^ bits) for i in range(devices)])  62.9 us
    pallas_call x2, Pallas kernels, scatter_add(): pl.pallas_call(functools.partial(scatter_body, len(pieces), nout, lots),...  51.6 us
    pallas_call x4, Pallas kernels, gather_sum(): pl.pallas_call(functools.partial(gather_body, len(tabs), len(dtypes), 8),...  50.1 us
    pallas_call x1, Pallas kernels, dense(): pl.pallas_call(functools.partial(dense_body, block, splits), out_shape=(j...  43.4 us
    convert_element_type x4, other arithmetic, reduce_blocks(): give = merged[i].astype(BF16)  8.92 us
  transfers between devices with their start and end apart: 54, of which 26 were waited for; matrix products, arithmetic and copies ran while one was open for 6% of the time, Pallas kernels for 26%

profile of v3, /device:TPU:0, one launch (start us, length us, event | category | flops | bytes accessed | tf_op | source)
XLA Modules:
  0.0 407.2 jit_solution(7552424004751066999)
XLA Ops:
  1.9 3.0 collective-permute-start.4
  6.4 2.6 collective-permute-start.1
  12.5 5.2 %collective-permute-done.4.refs_2_ = bf16[1024,256]{1,0:T(8,128)(2,1)S(1)} collective-permute-done((bf16[1024,256]{1,0:T(8,128)(2,1)S(1)}, bf16[1024,256]{1,0:T(8,128)(2,1)S(1)}, u32[]{:S(2)}, u32[]{:S(2)}) %collective-permute-start.4) | collective-permute-done | bytes 524320 | tf_op jit(solution)/shard_map/ppermute | solution.py:377
  18.5 4.1 %collective-permute-start.2 = (s32[4,1024]{1,0:T(4,128)S(1)}, s32[4,1024]{1,0:T(4,128)S(1)}, u32[]{:S(2)}, u32[]{:S(2)}) collective-permute-start(s32[4,1024]{1,0:T(4,128)S(1)} %get-tuple-element.62), channel_id=1, source_target_pairs={{0,24},{1,25},{2,26},{3,27},{4,28},{5,29},{6,30},{7,31},{8,16},{9,... | collective-permute-start | bytes 49160 | tf_op jit(solution)/shard_map/ppermute | solution.py:377
  24.4 1.7 collective-permute-start.13
  26.1 8.5 %collective-permute-done.6.refs_4_ = bf16[1024,256]{1,0:T(8,128)(2,1)S(1)} collective-permute-done((bf16[1024,256]{1,0:T(8,128)(2,1)S(1)}, bf16[1024,256]{1,0:T(8,128)(2,1)S(1)}, u32[]{:S(2)}, u32[]{:S(2)}) %collective-permute-start.6) | collective-permute-done | bytes 524320 | tf_op jit(solution)/shard_map/ppermute | solution.py:377
  39.5 17.0 %gather_sum.4 = (bf16[1024,256]{1,0:T(8,128)(2,1)}, bf16[1024,256]{1,0:T(8,128)(2,1)}, f32[1024,256]{1,0:T(8,128)}) custom-call(s32[12288]{0:T(1024)} %copy-done.36, bf16[1024,256]{1,0:T(8,128)(2,1)} %copy-done.3, bf16[1024,256]{1,0:T(8,128)(2,1)} %copy-done.10, bf16[1024,256]{1,0:T(8,128)(2,1)} %copy-done.4, bf16[1024,256]{1,0:T(8,128)(2,1)} %copy-done.11, ...), custom_call_target="tpu_custom_call" | custom-call | tf_op jit(solution)/shard_map/gather_sum/pallas_call | solution.py:275
  56.5 8.1 %gather_sum.5 = bf16[1024,256]{1,0:T(8,128)(2,1)} custom-call(s32[4096]{0:T(1024)} %bitcast.123, bf16[1024,256]{1,0:T(8,128)(2,1)} %copy-done.3, bf16[1024,256]{1,0:T(8,128)(2,1)} %copy-done.10, bf16[1024,256]{1,0:T(8,128)(2,1)} %copy-done.4, bf16[1024,256]{1,0:T(8,128)(2,1)} %copy-done.11, bf16[1024,256]{1,0:T(8,128)(2,1)} %copy-done.8, ...), custom_call_target="tpu_custom_call" | custom-call | tf_op jit(solution)/shard_map/gather_sum/pallas_call | solution.py:275
  69.0 8.1 %gather_sum.7 = bf16[1024,256]{1,0:T(8,128)(2,1)} custom-call(s32[4096]{0:T(1024)} %bitcast.124, bf16[1024,256]{1,0:T(8,128)(2,1)} %copy-done.2, bf16[1024,256]{1,0:T(8,128)(2,1)} %copy-done.12, bf16[1024,256]{1,0:T(8,128)(2,1)} %copy-done.5, bf16[1024,256]{1,0:T(8,128)(2,1)} %copy-done.13, bf16[1024,256]{1,0:T(8,128)(2,1)} %copy-done.6, ...), custom_call_target="tpu_custom_call" | custom-call | tf_op jit(solution)/shard_map/gather_sum/pallas_call | solution.py:275
  79.9 2.1 add_convert_fusion.3
  82.6 17.0 %gather_sum.6 = (bf16[1024,256]{1,0:T(8,128)(2,1)}, bf16[1024,256]{1,0:T(8,128)(2,1)}, f32[1024,256]{1,0:T(8,128)}) custom-call(s32[12288]{0:T(1024)} %copy-done.36, bf16[1024,256]{1,0:T(8,128)(2,1)} %copy-done.2, bf16[1024,256]{1,0:T(8,128)(2,1)} %copy-done.12, bf16[1024,256]{1,0:T(8,128)(2,1)} %copy-done.5, bf16[1024,256]{1,0:T(8,128)(2,1)} %copy-done.13, ...), custom_call_target="tpu_custom_call" | custom-call | tf_op jit(solution)/shard_map/gather_sum/pallas_call | solution.py:275
  99.6 1.7 collective-permute-start.20
  101.3 2.0 collective-permute-done.21
  103.3 2.0 add_convert_fusion.1
  106.3 19.5 %collective-permute-done.10 = bf16[1024,256]{1,0:T(8,128)(2,1)S(1)} collective-permute-done((bf16[1024,256]{1,0:T(8,128)(2,1)}, bf16[1024,256]{1,0:T(8,128)(2,1)S(1)}, u32[]{:S(2)}, u32[]{:S(2)}) %collective-permute-start.10) | collective-permute-done | bytes 524320 | tf_op jit(solution)/shard_map/ppermute | solution.py:377
  126.7 9.5 %collective-permute-done.20 = bf16[1024,256]{1,0:T(8,128)(2,1)} collective-permute-done((bf16[1024,256]{1,0:T(8,128)(2,1)}, bf16[1024,256]{1,0:T(8,128)(2,1)}, u32[]{:S(2)}, u32[]{:S(2)}) %collective-permute-start.20) | collective-permute-done | bytes 524320 | tf_op jit(solution)/shard_map/ppermute | solution.py:377
  136.3 2.2 add_convert_fusion.refs_1_
  138.4 43.4 %dense_step.1 = (bf16[1024,256]{1,0:T(8,128)(2,1)}, bf16[1024,256]{1,0:T(8,128)(2,1)}, bf16[1024,512]{1,0:T(8,128)(2,1)}, bf16[1024,512]{1,0:T(8,128)(2,1)}, bf16[1024,2048]{1,0:T(8,128)(2,1)}) custom-call(bf16[1024,256]{1,0:T(8,128)(2,1)} %add_convert_fusion.2.refs_0_, bf16[1024,256]{1,0:T(8,128)(2,1)} %add_convert_fusion.refs_1_, s32[1024,1]{1,0:T(8,128)} %copy.15.refs_2_, ...), custom_call_target="tpu_custom_call" | custom-call | tf_op jit(solution)/shard_map/dense_step/pallas_call | solution.py:189
  181.8 2.1 fusion.60
  184.3 3.7 fusion.59
  188.4 2.4 copy-done
  196.2 21.7 %collective-permute-done.24.refs_2_ = bf16[1024,256]{1,0:T(8,128)(2,1)} collective-permute-done((bf16[1024,256]{1,0:T(8,128)(2,1)}, bf16[1024,256]{1,0:T(8,128)(2,1)}, u32[]{:S(2)}, u32[]{:S(2)}) %collective-permute-start.24) | collective-permute-done | bytes 524320 | tf_op jit(solution)/shard_map/ppermute | solution.py:377
  217.9 2.2 collective-permute-start.32
  220.1 2.1 bitcast_add_fusion
  223.2 29.2 %collective-permute-done.30.refs_1_ = bf16[1024,256]{1,0:T(8,128)(2,1)} collective-permute-done((bf16[1024,256]{1,0:T(8,128)(2,1)}, bf16[1024,256]{1,0:T(8,128)(2,1)}, u32[]{:S(2)}, u32[]{:S(2)}) %collective-permute-start.30) | collective-permute-done | bytes 524320 | tf_op jit(solution)/shard_map/ppermute | solution.py:377
  256.7 25.8 %scatter_add.3 = (f32[1024,256]{1,0:T(8,128)}, bf16[1024,256]{1,0:T(8,128)(2,1)}, bf16[1024,256]{1,0:T(8,128)(2,1)}, bf16[1024,256]{1,0:T(8,128)(2,1)}, bf16[4,1024,256]{2,1,0:T(8,128)(2,1)}) custom-call(s32[16384]{0:T(1024)} %bitcast.120, bf16[1024,256]{1,0:T(8,128)(2,1)} %get-tuple-element.46.refs_0_, bf16[1024,256]{1,0:T(8,128)(2,1)} %collective-permute-done.30.refs_1_, ...), custom_call_target="tpu_custom_call" | custom-call | tf_op jit(solution)/shard_map/scatter_add/pallas_call | solution.py:334
  282.5 25.8 %scatter_add.2 = (f32[1024,256]{1,0:T(8,128)}, bf16[1024,256]{1,0:T(8,128)(2,1)}, bf16[1024,256]{1,0:T(8,128)(2,1)}, bf16[1024,256]{1,0:T(8,128)(2,1)}, bf16[4,1024,256]{2,1,0:T(8,128)(2,1)}) custom-call(s32[16384]{0:T(1024)} %bitcast.121, bf16[1024,256]{1,0:T(8,128)(2,1)} %get-tuple-element.40.refs_0_, bf16[1024,256]{1,0:T(8,128)(2,1)} %collective-permute-done.23.refs_1_, ...), custom_call_target="tpu_custom_call" | custom-call | tf_op jit(solution)/shard_map/scatter_add/pallas_call | solution.py:334
  310.9 9.7 %collective-permute-start.41 = (bf16[16,2560]{1,0:T(8,128)(2,1)S(1)}, bf16[16,2560]{1,0:T(8,128)(2,1)S(1)}, u32[]{:S(2)}, u32[]{:S(2)}) collective-permute-start(bf16[16,2560]{1,0:T(8,128)(2,1)S(1)} %get-tuple-element.83), channel_id=1, source_target_pairs={{0,8},{1,9},{2,10},{3,11},{4,12},{5,13},{6,14},{7,15},{8,0},{9,1},... | collective-permute-start | bytes 245768 | tf_op jit(solution)/shard_map/ppermute | solution.py:377
  320.6 2.4 collective-permute-start.43
  323.4 5.5 %collective-permute-done.42 = bf16[16,2560]{1,0:T(8,128)(2,1)S(1)} collective-permute-done((bf16[16,2560]{1,0:T(8,128)(2,1)S(1)}, bf16[16,2560]{1,0:T(8,128)(2,1)S(1)}, u32[]{:S(2)}, u32[]{:S(2)}) %collective-permute-start.42) | collective-permute-done | bytes 81952 | tf_op jit(solution)/shard_map/ppermute | solution.py:377
  329.0 1.9 fusion.48
  330.9 2.2 collective-permute-start.44
  333.1 2.4 collective-permute-start.46
  336.0 5.9 %collective-permute-done.45 = bf16[16,2560]{1,0:T(8,128)(2,1)S(1)} collective-permute-done((bf16[16,2560]{1,0:T(8,128)(2,1)S(1)}, bf16[16,2560]{1,0:T(8,128)(2,1)S(1)}, u32[]{:S(2)}, u32[]{:S(2)}) %collective-permute-start.45) | collective-permute-done | bytes 81952 | tf_op jit(solution)/shard_map/ppermute | solution.py:377
  343.1 2.4 collective-permute-start.49
  345.5 7.1 %collective-permute-done.47.refs_1_ = bf16[4,16,2560]{2,1,0:T(8,128)(2,1)S(1)} collective-permute-done((bf16[4,16,2560]{2,1,0:T(8,128)(2,1)S(1)}, bf16[4,16,2560]{2,1,0:T(8,128)(2,1)S(1)}, u32[]{:S(2)}, u32[]{:S(2)}) %collective-permute-start.47) | collective-permute-done | bytes 327712 | tf_op jit(solution)/shard_map/ppermute | solution.py:377
  353.1 2.0 fusion.3
  355.2 2.8 collective-permute-done.48.refs_2_
  358.0 1.7 collective-permute-start.34
  362.1 2.8 fusion.9
  364.9 1.7 collective-permute-start.27
  366.9 5.9 %collective-permute-done.34 = bf16[1024,256]{1,0:T(8,128)(2,1)S(1)} collective-permute-done((bf16[1024,256]{1,0:T(8,128)(2,1)S(1)}, bf16[1024,256]{1,0:T(8,128)(2,1)S(1)}, u32[]{:S(2)}, u32[]{:S(2)}) %collective-permute-start.34) | collective-permute-done | bytes 524320 | tf_op jit(solution)/shard_map/ppermute | solution.py:377
  374.3 3.4 place_blocks.1
  377.7 5.7 %collective-permute-done.35 = bf16[1024,256]{1,0:T(8,128)(2,1)} collective-permute-done((bf16[1024,256]{1,0:T(8,128)(2,1)S(1)}, bf16[1024,256]{1,0:T(8,128)(2,1)}, u32[]{:S(2)}, u32[]{:S(2)}) %collective-permute-start.35) | collective-permute-done | bytes 524320 | tf_op jit(solution)/shard_map/ppermute | solution.py:377
  385.2 10.2 %collective-permute-done.27 = bf16[1024,256]{1,0:T(8,128)(2,1)} collective-permute-done((bf16[1024,256]{1,0:T(8,128)(2,1)}, bf16[1024,256]{1,0:T(8,128)(2,1)}, u32[]{:S(2)}, u32[]{:S(2)}) %collective-permute-start.27) | collective-permute-done | bytes 524320 | tf_op jit(solution)/shard_map/ppermute | solution.py:377
  395.4 8.3 %collective-permute-done.28 = bf16[1024,256]{1,0:T(8,128)(2,1)} collective-permute-done((bf16[1024,256]{1,0:T(8,128)(2,1)}, bf16[1024,256]{1,0:T(8,128)(2,1)}, u32[]{:S(2)}, u32[]{:S(2)}) %collective-permute-start.28) | collective-permute-done | bytes 524320 | tf_op jit(solution)/shard_map/ppermute | solution.py:377
  403.7 1.8 fusion.12
  405.5 1.6 pad_maximum_fusion.1
  (193 shorter events, 45.7 us)
Async XLA Ops:
  1.9 15.8 %collective-permute-start.4 = (bf16[1024,256]{1,0:T(8,128)(2,1)S(1)}, bf16[1024,256]{1,0:T(8,128)(2,1)S(1)}, u32[]{:S(2)}, u32[]{:S(2)}) collective-permute-start(bf16[1024,256]{1,0:T(8,128)(2,1)S(1)} %get-tuple-element.82.refs_0_), channel_id=1, source_target_pairs={{0,2},{1,3},{2,0},{3,1},{4,6},{5,7},{6,4},{7,5},{8,10},{9,11},{10,... | collective-permute-start | bytes 1572872 | tf_op jit(solution)/shard_map/ppermute | solution.py:377
  6.4 6.2 %collective-permute-start.1 = (s32[4,1024]{1,0:T(4,128)S(1)}, s32[4,1024]{1,0:T(4,128)S(1)}, u32[]{:S(2)}, u32[]{:S(2)}) collective-permute-start(s32[4,1024]{1,0:T(4,128)S(1)} %get-tuple-element.62), channel_id=1, source_target_pairs={{0,16},{1,17},{2,18},{3,19},{4,20},{5,21},{6,22},{7,23},{8,24},{9,... | collective-permute-start | bytes 49160 | tf_op jit(solution)/shard_map/ppermute | solution.py:377
  9.0 9.5 %collective-permute-start = (s32[4,1024]{1,0:T(4,128)S(1)}, s32[4,1024]{1,0:T(4,128)S(1)}, u32[]{:S(2)}, u32[]{:S(2)}) collective-permute-start(s32[4,1024]{1,0:T(4,128)S(1)} %get-tuple-element.62), channel_id=1, source_target_pairs={{0,8},{1,9},{2,10},{3,11},{4,12},{5,13},{6,14},{7,15},{8,0},{9,1},... | collective-permute-start | bytes 49160 | tf_op jit(solution)/shard_map/ppermute | solution.py:377
  10.5 24.1 %collective-permute-start.6 = (bf16[1024,256]{1,0:T(8,128)(2,1)S(1)}, bf16[1024,256]{1,0:T(8,128)(2,1)S(1)}, u32[]{:S(2)}, u32[]{:S(2)}) collective-permute-start(bf16[1024,256]{1,0:T(8,128)(2,1)S(1)} %get-tuple-element.82.refs_0_), channel_id=1, source_target_pairs={{0,4},{1,5},{2,6},{3,7},{4,0},{5,1},{6,2},{7,3},{8,12},{9,13},{10,... | collective-permute-start | bytes 1572872 | tf_op jit(solution)/shard_map/ppermute | solution.py:377
  12.1 24.1 %collective-permute-start.8 = (bf16[1024,256]{1,0:T(8,128)(2,1)S(1)}, bf16[1024,256]{1,0:T(8,128)(2,1)S(1)}, u32[]{:S(2)}, u32[]{:S(2)}) collective-permute-start(bf16[1024,256]{1,0:T(8,128)(2,1)S(1)} %get-tuple-element.82.refs_0_), channel_id=1, source_target_pairs={{0,6},{1,7},{2,4},{3,5},{4,2},{5,3},{6,0},{7,1},{8,14},{9,15},{10,... | collective-permute-start | bytes 1572872 | tf_op jit(solution)/shard_map/ppermute | solution.py:377
  12.5 24.1 %collective-permute-start.3 = (bf16[1024,256]{1,0:T(8,128)(2,1)S(1)}, bf16[1024,256]{1,0:T(8,128)(2,1)S(1)}, u32[]{:S(2)}, u32[]{:S(2)}) collective-permute-start(bf16[1024,256]{1,0:T(8,128)(2,1)S(1)} %get-tuple-element.82.refs_0_), channel_id=1, source_target_pairs={{0,1},{1,0},{2,3},{3,2},{4,5},{5,4},{6,7},{7,6},{8,9},{9,8},{10,11... | collective-permute-start | bytes 1572872 | tf_op jit(solution)/shard_map/ppermute | solution.py:377
  17.7 18.9 %collective-permute-start.5 = (bf16[1024,256]{1,0:T(8,128)(2,1)S(1)}, bf16[1024,256]{1,0:T(8,128)(2,1)S(1)}, u32[]{:S(2)}, u32[]{:S(2)}) collective-permute-start(bf16[1024,256]{1,0:T(8,128)(2,1)S(1)} %collective-permute-done.4.refs_2_), channel_id=1, source_target_pairs={{0,1},{1,0},{2,3},{3,2},{4,5},{5,4},{6,7},{7,6},{8,9},{9,8},{10,11... | collective-permute-start | bytes 1572872 | tf_op jit(solution)/shard_map/ppermute | solution.py:377
  18.5 5.8 %collective-permute-start.2 = (s32[4,1024]{1,0:T(4,128)S(1)}, s32[4,1024]{1,0:T(4,128)S(1)}, u32[]{:S(2)}, u32[]{:S(2)}) collective-permute-start(s32[4,1024]{1,0:T(4,128)S(1)} %get-tuple-element.62), channel_id=1, source_target_pairs={{0,24},{1,25},{2,26},{3,27},{4,28},{5,29},{6,30},{7,31},{8,16},{9,... | collective-permute-start | bytes 49160 | tf_op jit(solution)/shard_map/ppermute | solution.py:377
  24.4 40.2 %collective-permute-start.13 = (bf16[1024,256]{1,0:T(8,128)(2,1)S(1)}, bf16[1024,256]{1,0:T(8,128)(2,1)S(1)}, u32[]{:S(2)}, u32[]{:S(2)}) collective-permute-start(bf16[1024,256]{1,0:T(8,128)(2,1)S(1)} %get-tuple-element.33.refs_0_), channel_id=1, source_target_pairs={{0,2},{1,3},{2,0},{3,1},{4,6},{5,7},{6,4},{7,5},{8,10},{9,11},{10,... | collective-permute-start | bytes 1572872 | tf_op jit(solution)/shard_map/ppermute | solution.py:377
  34.6 29.9 %collective-permute-start.14 = (bf16[1024,256]{1,0:T(8,128)(2,1)S(1)}, bf16[1024,256]{1,0:T(8,128)(2,1)S(1)}, u32[]{:S(2)}, u32[]{:S(2)}) collective-permute-start(bf16[1024,256]{1,0:T(8,128)(2,1)S(1)} %get-tuple-element.33.refs_0_), channel_id=1, source_target_pairs={{0,4},{1,5},{2,6},{3,7},{4,0},{5,1},{6,2},{7,3},{8,12},{9,13},{10,... | collective-permute-start | bytes 1572872 | tf_op jit(solution)/shard_map/ppermute | solution.py:377
  36.1 28.4 %collective-permute-start.15 = (bf16[1024,256]{1,0:T(8,128)(2,1)S(1)}, bf16[1024,256]{1,0:T(8,128)(2,1)S(1)}, u32[]{:S(2)}, u32[]{:S(2)}) collective-permute-start(bf16[1024,256]{1,0:T(8,128)(2,1)S(1)} %get-tuple-element.33.refs_0_), channel_id=1, source_target_pairs={{0,6},{1,7},{2,4},{3,5},{4,2},{5,3},{6,0},{7,1},{8,14},{9,15},{10,... | collective-permute-start | bytes 1572872 | tf_op jit(solution)/shard_map/ppermute | solution.py:377
  65.3 3.7 collective-permute-start.19
  65.7 14.3 %collective-permute-start.11 = (bf16[1024,256]{1,0:T(8,128)(2,1)}, bf16[1024,256]{1,0:T(8,128)(2,1)}, u32[]{:S(2)}, u32[]{:S(2)}) collective-permute-start(bf16[1024,256]{1,0:T(8,128)(2,1)} %gather_sum.5), channel_id=1, source_target_pairs={{0,8},{1,9},{2,10},{3,11},{4,12},{5,13},{6,14},{7,15},{8,0},{9,1},... | collective-permute-start | bytes 1572872 | tf_op jit(solution)/shard_map/ppermute | solution.py:377
  77.0 26.2 %collective-permute-start.21 = (bf16[1024,256]{1,0:T(8,128)(2,1)}, bf16[1024,256]{1,0:T(8,128)(2,1)S(1)}, u32[]{:S(2)}, u32[]{:S(2)}) collective-permute-start(bf16[1024,256]{1,0:T(8,128)(2,1)} %gather_sum.7), channel_id=1, source_target_pairs={{0,8},{1,9},{2,10},{3,11},{4,12},{5,13},{6,14},{7,15},{8,0},{9,1},... | collective-permute-start | bytes 1572872 | tf_op jit(solution)/shard_map/ppermute | solution.py:377
  77.5 48.3 %collective-permute-start.10 = (bf16[1024,256]{1,0:T(8,128)(2,1)}, bf16[1024,256]{1,0:T(8,128)(2,1)S(1)}, u32[]{:S(2)}, u32[]{:S(2)}) collective-permute-start(bf16[1024,256]{1,0:T(8,128)(2,1)} %get-tuple-element.31), channel_id=1, source_target_pairs={{0,8},{1,9},{2,10},{3,11},{4,12},{5,13},{6,14},{7,15},{8,0},{9,1},... | collective-permute-start | bytes 1572872 | tf_op jit(solution)/shard_map/ppermute | solution.py:377
  82.1 43.7 %collective-permute-start.12 = (bf16[1024,256]{1,0:T(8,128)(2,1)}, bf16[1024,256]{1,0:T(8,128)(2,1)S(1)}, u32[]{:S(2)}, u32[]{:S(2)}) collective-permute-start(bf16[1024,256]{1,0:T(8,128)(2,1)} %add_convert_fusion.3), channel_id=1, source_target_pairs={{0,16},{1,17},{2,18},{3,19},{4,20},{5,21},{6,22},{7,23},{8,24},{9,... | collective-permute-start | bytes 1572872 | tf_op jit(solution)/shard_map/ppermute | solution.py:377
  99.6 36.7 %collective-permute-start.20 = (bf16[1024,256]{1,0:T(8,128)(2,1)}, bf16[1024,256]{1,0:T(8,128)(2,1)}, u32[]{:S(2)}, u32[]{:S(2)}) collective-permute-start(bf16[1024,256]{1,0:T(8,128)(2,1)} %get-tuple-element.38), channel_id=1, source_target_pairs={{0,8},{1,9},{2,10},{3,11},{4,12},{5,13},{6,14},{7,15},{8,0},{9,1},... | collective-permute-start | bytes 1572872 | tf_op jit(solution)/shard_map/ppermute | solution.py:377
  105.3 31.0 %collective-permute-start.22 = (bf16[1024,256]{1,0:T(8,128)(2,1)}, bf16[1024,256]{1,0:T(8,128)(2,1)}, u32[]{:S(2)}, u32[]{:S(2)}) collective-permute-start(bf16[1024,256]{1,0:T(8,128)(2,1)} %add_convert_fusion.1), channel_id=1, source_target_pairs={{0,16},{1,17},{2,18},{3,19},{4,20},{5,21},{6,22},{7,23},{8,24},{9,... | collective-permute-start | bytes 1572872 | tf_op jit(solution)/shard_map/ppermute | solution.py:377
  191.0 29.1 %collective-permute-start.37 = (bf16[4,4,16,2560]{3,2,0,1:T(8,128)(2,1)S(1)}, bf16[4,4,16,2560]{3,2,0,1:T(8,128)(2,1)S(1)}, u32[]{:S(2)}, u32[]{:S(2)}) collective-permute-start(bf16[4,4,16,2560]{3,2,0,1:T(8,128)(2,1)S(1)} %fusion), channel_id=1, source_target_pairs={{0,1},{1,0},{2,3},{3,2},{4,5},{5,4},{6,7},{7,6},{8,9},{9,8},{10,11... | collective-permute-start | bytes 3932168 | tf_op jit(solution)/shard_map/ppermute | solution.py:377
  191.1 26.9 %collective-permute-start.24 = (bf16[1024,256]{1,0:T(8,128)(2,1)}, bf16[1024,256]{1,0:T(8,128)(2,1)}, u32[]{:S(2)}, u32[]{:S(2)}) collective-permute-start(bf16[1024,256]{1,0:T(8,128)(2,1)} %get-tuple-element.40.refs_0_), channel_id=1, source_target_pairs={{0,16},{1,17},{2,18},{3,19},{4,20},{5,21},{6,22},{7,23},{8,24},{9,... | collective-permute-start | bytes 1572872 | tf_op jit(solution)/shard_map/ppermute | solution.py:377
  192.5 90.0 %collective-permute-start.23 = (bf16[1024,256]{1,0:T(8,128)(2,1)}, bf16[1024,256]{1,0:T(8,128)(2,1)}, u32[]{:S(2)}, u32[]{:S(2)}) collective-permute-start(bf16[1024,256]{1,0:T(8,128)(2,1)} %get-tuple-element.40.refs_0_), channel_id=1, source_target_pairs={{0,8},{1,9},{2,10},{3,11},{4,12},{5,13},{6,14},{7,15},{8,0},{9,1},... | collective-permute-start | bytes 1572872 | tf_op jit(solution)/shard_map/ppermute | solution.py:377
  193.4 59.1 %collective-permute-start.30 = (bf16[1024,256]{1,0:T(8,128)(2,1)}, bf16[1024,256]{1,0:T(8,128)(2,1)}, u32[]{:S(2)}, u32[]{:S(2)}) collective-permute-start(bf16[1024,256]{1,0:T(8,128)(2,1)} %get-tuple-element.46.refs_0_), channel_id=1, source_target_pairs={{0,8},{1,9},{2,10},{3,11},{4,12},{5,13},{6,14},{7,15},{8,0},{9,1},... | collective-permute-start | bytes 1572872 | tf_op jit(solution)/shard_map/ppermute | solution.py:377
  194.6 59.3 %collective-permute-start.31 = (bf16[1024,256]{1,0:T(8,128)(2,1)}, bf16[1024,256]{1,0:T(8,128)(2,1)}, u32[]{:S(2)}, u32[]{:S(2)}) collective-permute-start(bf16[1024,256]{1,0:T(8,128)(2,1)} %get-tuple-element.46.refs_0_), channel_id=1, source_target_pairs={{0,16},{1,17},{2,18},{3,19},{4,20},{5,21},{6,22},{7,23},{8,24},{9,... | collective-permute-start | bytes 1572872 | tf_op jit(solution)/shard_map/ppermute | solution.py:377
  217.9 37.5 %collective-permute-start.32 = (bf16[1024,256]{1,0:T(8,128)(2,1)}, bf16[1024,256]{1,0:T(8,128)(2,1)}, u32[]{:S(2)}, u32[]{:S(2)}) collective-permute-start(bf16[1024,256]{1,0:T(8,128)(2,1)} %get-tuple-element.46.refs_0_), channel_id=1, source_target_pairs={{0,24},{1,25},{2,26},{3,27},{4,28},{5,29},{6,30},{7,31},{8,16},{9,... | collective-permute-start | bytes 1572872 | tf_op jit(solution)/shard_map/ppermute | solution.py:377
  220.1 62.4 %collective-permute-start.25 = (bf16[1024,256]{1,0:T(8,128)(2,1)}, bf16[1024,256]{1,0:T(8,128)(2,1)}, u32[]{:S(2)}, u32[]{:S(2)}) collective-permute-start(bf16[1024,256]{1,0:T(8,128)(2,1)} %collective-permute-done.24.refs_2_), channel_id=1, source_target_pairs={{0,8},{1,9},{2,10},{3,11},{4,12},{5,13},{6,14},{7,15},{8,0},{9,1},... | collective-permute-start | bytes 1572872 | tf_op jit(solution)/shard_map/ppermute | solution.py:377
  252.5 56.4 %collective-permute-start.38 = (bf16[4,16,2560]{2,1,0:T(8,128)(2,1)}, bf16[4,16,2560]{2,1,0:T(8,128)(2,1)S(1)}, u32[]{:S(2)}, u32[]{:S(2)}) collective-permute-start(bf16[4,16,2560]{2,1,0:T(8,128)(2,1)} %get-tuple-element.72), channel_id=1, source_target_pairs={{0,2},{1,3},{2,0},{3,1},{4,6},{5,7},{6,4},{7,5},{8,10},{9,11},{10,... | collective-permute-start | bytes 983048 | tf_op jit(solution)/shard_map/ppermute | solution.py:377
  253.9 54.9 %collective-permute-start.39 = (bf16[4,16,2560]{2,1,0:T(8,128)(2,1)}, bf16[4,16,2560]{2,1,0:T(8,128)(2,1)S(1)}, u32[]{:S(2)}, u32[]{:S(2)}) collective-permute-start(bf16[4,16,2560]{2,1,0:T(8,128)(2,1)} %get-tuple-element.74), channel_id=1, source_target_pairs={{0,4},{1,5},{2,6},{3,7},{4,0},{5,1},{6,2},{7,3},{8,12},{9,13},{10,... | collective-permute-start | bytes 983048 | tf_op jit(solution)/shard_map/ppermute | solution.py:377
  255.4 54.2 %collective-permute-start.40 = (bf16[4,16,2560]{2,1,0:T(8,128)(2,1)S(1)}, bf16[4,16,2560]{2,1,0:T(8,128)(2,1)}, u32[]{:S(2)}, u32[]{:S(2)}) collective-permute-start(bf16[4,16,2560]{2,1,0:T(8,128)(2,1)S(1)} %get-tuple-element.73), channel_id=1, source_target_pairs={{0,6},{1,7},{2,4},{3,5},{4,2},{5,3},{6,0},{7,1},{8,14},{9,15},{10,... | collective-permute-start | bytes 983048 | tf_op jit(solution)/shard_map/ppermute | solution.py:377
  282.5 70.1 %collective-permute-start.33 = (bf16[4,1024,256]{2,1,0:T(8,128)(2,1)}, bf16[4,1024,256]{2,1,0:T(8,128)(2,1)}, u32[]{:S(2)}, u32[]{:S(2)}) collective-permute-start(bf16[4,1024,256]{2,1,0:T(8,128)(2,1)} %get-tuple-element.48), channel_id=1, source_target_pairs={{0,1},{1,0},{2,3},{3,2},{4,5},{5,4},{6,7},{7,6},{8,9},{9,8},{10,11... | collective-permute-start | bytes 6291464 | tf_op jit(solution)/shard_map/ppermute | solution.py:377
  308.3 53.2 %collective-permute-start.26 = (bf16[4,1024,256]{2,1,0:T(8,128)(2,1)}, bf16[4,1024,256]{2,1,0:T(8,128)(2,1)}, u32[]{:S(2)}, u32[]{:S(2)}) collective-permute-start(bf16[4,1024,256]{2,1,0:T(8,128)(2,1)} %get-tuple-element.42), channel_id=1, source_target_pairs={{0,1},{1,0},{2,3},{3,2},{4,5},{5,4},{6,7},{7,6},{8,9},{9,8},{10,11... | collective-permute-start | bytes 6291464 | tf_op jit(solution)/shard_map/ppermute | solution.py:377
  310.9 12.5 %collective-permute-start.41 = (bf16[16,2560]{1,0:T(8,128)(2,1)S(1)}, bf16[16,2560]{1,0:T(8,128)(2,1)S(1)}, u32[]{:S(2)}, u32[]{:S(2)}) collective-permute-start(bf16[16,2560]{1,0:T(8,128)(2,1)S(1)} %get-tuple-element.83), channel_id=1, source_target_pairs={{0,8},{1,9},{2,10},{3,11},{4,12},{5,13},{6,14},{7,15},{8,0},{9,1},... | collective-permute-start | bytes 245768 | tf_op jit(solution)/shard_map/ppermute | solution.py:377
  320.6 8.4 %collective-permute-start.42 = (bf16[16,2560]{1,0:T(8,128)(2,1)S(1)}, bf16[16,2560]{1,0:T(8,128)(2,1)S(1)}, u32[]{:S(2)}, u32[]{:S(2)}) collective-permute-start(bf16[16,2560]{1,0:T(8,128)(2,1)S(1)} %get-tuple-element.85), channel_id=1, source_target_pairs={{0,16},{1,17},{2,18},{3,19},{4,20},{5,21},{6,22},{7,23},{8,24},{9,... | collective-permute-start | bytes 245768 | tf_op jit(solution)/shard_map/ppermute | solution.py:377
  320.6 8.4 %collective-permute-start.43 = (bf16[16,2560]{1,0:T(8,128)(2,1)S(1)}, bf16[16,2560]{1,0:T(8,128)(2,1)S(1)}, u32[]{:S(2)}, u32[]{:S(2)}) collective-permute-start(bf16[16,2560]{1,0:T(8,128)(2,1)S(1)} %get-tuple-element.84), channel_id=1, source_target_pairs={{0,24},{1,25},{2,26},{3,27},{4,28},{5,29},{6,30},{7,31},{8,16},{9,... | collective-permute-start | bytes 245768 | tf_op jit(solution)/shard_map/ppermute | solution.py:377
  330.9 5.1 %collective-permute-start.44 = (bf16[16,2560]{1,0:T(8,128)(2,1)S(1)}, bf16[16,2560]{1,0:T(8,128)(2,1)S(1)}, u32[]{:S(2)}, u32[]{:S(2)}) collective-permute-start(bf16[16,2560]{1,0:T(8,128)(2,1)S(1)} %get-tuple-element.55), channel_id=1, source_target_pairs={{0,8},{1,9},{2,10},{3,11},{4,12},{5,13},{6,14},{7,15},{8,0},{9,1},... | collective-permute-start | bytes 245768 | tf_op jit(solution)/shard_map/ppermute | solution.py:377
  333.1 8.8 %collective-permute-start.45 = (bf16[16,2560]{1,0:T(8,128)(2,1)S(1)}, bf16[16,2560]{1,0:T(8,128)(2,1)S(1)}, u32[]{:S(2)}, u32[]{:S(2)}) collective-permute-start(bf16[16,2560]{1,0:T(8,128)(2,1)S(1)} %get-tuple-element.55), channel_id=1, source_target_pairs={{0,16},{1,17},{2,18},{3,19},{4,20},{5,21},{6,22},{7,23},{8,24},{9,... | collective-permute-start | bytes 245768 | tf_op jit(solution)/shard_map/ppermute | solution.py:377
  333.1 8.8 %collective-permute-start.46 = (bf16[16,2560]{1,0:T(8,128)(2,1)S(1)}, bf16[16,2560]{1,0:T(8,128)(2,1)S(1)}, u32[]{:S(2)}, u32[]{:S(2)}) collective-permute-start(bf16[16,2560]{1,0:T(8,128)(2,1)S(1)} %get-tuple-element.55), channel_id=1, source_target_pairs={{0,24},{1,25},{2,26},{3,27},{4,28},{5,29},{6,30},{7,31},{8,16},{9,... | collective-permute-start | bytes 245768 | tf_op jit(solution)/shard_map/ppermute | solution.py:377
  342.0 10.6 %collective-permute-start.47 = (bf16[4,16,2560]{2,1,0:T(8,128)(2,1)S(1)}, bf16[4,16,2560]{2,1,0:T(8,128)(2,1)S(1)}, u32[]{:S(2)}, u32[]{:S(2)}) collective-permute-start(bf16[4,16,2560]{2,1,0:T(8,128)(2,1)S(1)} %pad_maximum_fusion.2.refs_0_), channel_id=1, source_target_pairs={{0,2},{1,3},{2,0},{3,1},{4,6},{5,7},{6,4},{7,5},{8,10},{9,11},{10,... | collective-permute-start | bytes 983048 | tf_op jit(solution)/shard_map/ppermute | solution.py:377
  342.9 15.1 %collective-permute-start.48 = (bf16[4,16,2560]{2,1,0:T(8,128)(2,1)S(1)}, bf16[4,16,2560]{2,1,0:T(8,128)(2,1)S(1)}, u32[]{:S(2)}, u32[]{:S(2)}) collective-permute-start(bf16[4,16,2560]{2,1,0:T(8,128)(2,1)S(1)} %pad_maximum_fusion.2.refs_0_), channel_id=1, source_target_pairs={{0,4},{1,5},{2,6},{3,7},{4,0},{5,1},{6,2},{7,3},{8,12},{9,13},{10,... | collective-permute-start | bytes 983048 | tf_op jit(solution)/shard_map/ppermute | solution.py:377
  343.1 16.6 %collective-permute-start.49 = (bf16[4,16,2560]{2,1,0:T(8,128)(2,1)S(1)}, bf16[4,16,2560]{2,1,0:T(8,128)(2,1)S(1)}, u32[]{:S(2)}, u32[]{:S(2)}) collective-permute-start(bf16[4,16,2560]{2,1,0:T(8,128)(2,1)S(1)} %pad_maximum_fusion.2.refs_0_), channel_id=1, source_target_pairs={{0,6},{1,7},{2,4},{3,5},{4,2},{5,3},{6,0},{7,1},{8,14},{9,15},{10,... | collective-permute-start | bytes 983048 | tf_op jit(solution)/shard_map/ppermute | solution.py:377
  352.6 7.4 %collective-permute-start.50 = (bf16[4,16,2560]{2,1,0:T(8,128)(2,1)S(1)}, bf16[4,16,2560]{2,1,0:T(8,128)(2,1)S(1)}, u32[]{:S(2)}, u32[]{:S(2)}) collective-permute-start(bf16[4,16,2560]{2,1,0:T(8,128)(2,1)S(1)} %pad_maximum_fusion.2.refs_0_), channel_id=1, source_target_pairs={{0,1},{1,0},{2,3},{3,2},{4,5},{5,4},{6,7},{7,6},{8,9},{9,8},{10,11... | collective-permute-start | bytes 983048 | tf_op jit(solution)/shard_map/ppermute | solution.py:377
  352.6 8.9 %collective-permute-start.51 = (bf16[4,16,2560]{2,1,0:T(8,128)(2,1)S(1)}, bf16[4,16,2560]{2,1,0:T(8,128)(2,1)S(1)}, u32[]{:S(2)}, u32[]{:S(2)}) collective-permute-start(bf16[4,16,2560]{2,1,0:T(8,128)(2,1)S(1)} %collective-permute-done.47.refs_1_), channel_id=1, source_target_pairs={{0,1},{1,0},{2,3},{3,2},{4,5},{5,4},{6,7},{7,6},{8,9},{9,8},{10,11... | collective-permute-start | bytes 983048 | tf_op jit(solution)/shard_map/ppermute | solution.py:377
  358.0 14.8 %collective-permute-start.34 = (bf16[1024,256]{1,0:T(8,128)(2,1)S(1)}, bf16[1024,256]{1,0:T(8,128)(2,1)S(1)}, u32[]{:S(2)}, u32[]{:S(2)}) collective-permute-start(bf16[1024,256]{1,0:T(8,128)(2,1)S(1)} %get-tuple-element.78), channel_id=1, source_target_pairs={{0,2},{1,3},{2,0},{3,1},{4,6},{5,7},{6,4},{7,5},{8,10},{9,11},{10,... | collective-permute-start | bytes 1572872 | tf_op jit(solution)/shard_map/ppermute | solution.py:377
  359.7 23.7 %collective-permute-start.35 = (bf16[1024,256]{1,0:T(8,128)(2,1)S(1)}, bf16[1024,256]{1,0:T(8,128)(2,1)}, u32[]{:S(2)}, u32[]{:S(2)}) collective-permute-start(bf16[1024,256]{1,0:T(8,128)(2,1)S(1)} %get-tuple-element.80), channel_id=1, source_target_pairs={{0,4},{1,5},{2,6},{3,7},{4,0},{5,1},{6,2},{7,3},{8,12},{9,13},{10,... | collective-permute-start | bytes 1572872 | tf_op jit(solution)/shard_map/ppermute | solution.py:377
  360.0 23.6 %collective-permute-start.36 = (bf16[1024,256]{1,0:T(8,128)(2,1)S(1)}, bf16[1024,256]{1,0:T(8,128)(2,1)}, u32[]{:S(2)}, u32[]{:S(2)}) collective-permute-start(bf16[1024,256]{1,0:T(8,128)(2,1)S(1)} %get-tuple-element.79), channel_id=1, source_target_pairs={{0,6},{1,7},{2,4},{3,5},{4,2},{5,3},{6,0},{7,1},{8,14},{9,15},{10,... | collective-permute-start | bytes 1572872 | tf_op jit(solution)/shard_map/ppermute | solution.py:377
  361.5 5.1 %collective-permute-start.53 = (bf16[4,16,2560]{2,1,0:T(8,128)(2,1)S(1)}, bf16[4,16,2560]{2,1,0:T(8,128)(2,1)S(1)}, u32[]{:S(2)}, u32[]{:S(2)}) collective-permute-start(bf16[4,16,2560]{2,1,0:T(8,128)(2,1)S(1)} %collective-permute-done.49.refs_3_), channel_id=1, source_target_pairs={{0,1},{1,0},{2,3},{3,2},{4,5},{5,4},{6,7},{7,6},{8,9},{9,8},{10,11... | collective-permute-start | bytes 983048 | tf_op jit(solution)/shard_map/ppermute | solution.py:377
  364.9 30.6 %collective-permute-start.27 = (bf16[1024,256]{1,0:T(8,128)(2,1)}, bf16[1024,256]{1,0:T(8,128)(2,1)}, u32[]{:S(2)}, u32[]{:S(2)}) collective-permute-start(bf16[1024,256]{1,0:T(8,128)(2,1)} %get-tuple-element.75), channel_id=1, source_target_pairs={{0,2},{1,3},{2,0},{3,1},{4,6},{5,7},{6,4},{7,5},{8,10},{9,11},{10,... | collective-permute-start | bytes 1572872 | tf_op jit(solution)/shard_map/ppermute | solution.py:377
  366.6 37.1 %collective-permute-start.28 = (bf16[1024,256]{1,0:T(8,128)(2,1)}, bf16[1024,256]{1,0:T(8,128)(2,1)}, u32[]{:S(2)}, u32[]{:S(2)}) collective-permute-start(bf16[1024,256]{1,0:T(8,128)(2,1)} %get-tuple-element.77), channel_id=1, source_target_pairs={{0,4},{1,5},{2,6},{3,7},{4,0},{5,1},{6,2},{7,3},{8,12},{9,13},{10,... | collective-permute-start | bytes 1572872 | tf_op jit(solution)/shard_map/ppermute | solution.py:377
  372.8 30.9 %collective-permute-start.29 = (bf16[1024,256]{1,0:T(8,128)(2,1)S(1)}, bf16[1024,256]{1,0:T(8,128)(2,1)}, u32[]{:S(2)}, u32[]{:S(2)}) collective-permute-start(bf16[1024,256]{1,0:T(8,128)(2,1)S(1)} %get-tuple-element.76), channel_id=1, source_target_pairs={{0,6},{1,7},{2,4},{3,5},{4,2},{5,3},{6,0},{7,1},{8,14},{9,15},{10,... | collective-permute-start | bytes 1572872 | tf_op jit(solution)/shard_map/ppermute | solution.py:377
  (52 other events, 1082.9 us)
